TPU v7x, 16 devices: a whole 2x2x2 slice. The times are simulated.
16 devices in a mesh: dp: 1, tp: 16 (over x, y, z, core).
Axes of the slice: x: 2, y: 2, z: 2, core: 2. Of those that a mesh axis runs over, the one named last changes fastest.
Arguments:
- x: bfloat16 [3072, 6144], P(('dp', 'tp'))
- w: bfloat16 [6144, 32768], P(None, 'tp')
- label: int32 [3072], P(('dp', 'tp'))
Outputs:
- output 1: float32 [3072], P(('dp', 'tp'))
- output 2: bfloat16 [3072, 6144], P(('dp', 'tp'))
- output 3: bfloat16 [6144, 32768], P('dp', 'tp')
All inputs are finite; a program needn't handle non-finite values.
Results may differ from a plain program's by a relative error of at most 0.012.
Values are sent between devices in bfloat16 or wider.
A program may use at most 2 GiB of HBM per device.

v0:
```python
import jax
import jax.numpy as jnp
from jax import lax
from jax.sharding import PartitionSpec as P


def solution(mesh):
    def step(x, w, label):
        me, own_rows, columns = lax.axis_index("tp"), x.shape[0], w.shape[1]
        rows = lax.all_gather(x, "tp", axis=0, tiled=True)
        wanted = lax.all_gather(label, "tp", axis=0, tiled=True)
        logits = jnp.dot(rows, w, preferred_element_type=jnp.float32)
        hit = (wanted - me * columns)[:, None] == jnp.arange(columns, dtype=jnp.int32)[None, :]
        high = jnp.max(logits, -1)
        own = jnp.stack([high, jnp.sum(jnp.exp(logits - high[:, None]), -1), jnp.sum(jnp.where(hit, logits, 0.0), -1)])
        high, sums, right = jnp.moveaxis(lax.all_gather(own, "tp"), 1, 0)
        top = jnp.max(high, 0)
        total = jnp.sum(sums * jnp.exp(high - top), 0)
        loss = jnp.log(total) + top - jnp.sum(right, 0)
        e = jnp.exp(logits - top[:, None])
        by_logits = (e / total[:, None] - hit.astype(jnp.float32)).astype(jnp.bfloat16)
        term = jnp.dot(by_logits, w.T, preferred_element_type=jnp.float32).astype(jnp.bfloat16)
        by_x = lax.psum_scatter(term, "tp", scatter_dimension=0, tiled=True)
        by_w = jnp.dot(rows.T, by_logits, preferred_element_type=jnp.float32).astype(jnp.bfloat16)
        return lax.dynamic_slice_in_dim(loss, me * own_rows, own_rows), by_x, by_w

    return jax.shard_map(
        step,
        mesh=mesh,
        in_specs=(P(("dp", "tp"), None), P(None, "tp"), P(("dp", "tp"))),
        out_specs=(P(("dp", "tp")), P(("dp", "tp"), None), P("dp", "tp")),
        check_vma=False,
    )
```

profile of v0, /device:TPU:0, one launch (start us, length us, event | category | flops | bytes accessed | tf_op | source)
XLA Modules:
  0.0 573.7 jit_solution(4448931915515356503)
XLA Ops:
  7.2 0.0 all-gather.4.cloned.1.call-start
  7.2 0.7 all-gather.4.cloned.1.call-update
  7.9 0.0 reduce-scatter.2.cloned.1.call-start
  8.0 0.9 dynamic-update-slice
  8.9 35.4 %all-reduce = s32[3072]{0:T(1024)S(1)} all-reduce(s32[3072]{0:T(1024)S(1)} %dynamic-update-slice), channel_id=1, replica_groups=mesh['dp'=1,'tp'=16] {'tp'}, use_global_device_ids=true, to_apply=%add | all-reduce | flops 3072 | bytes 24576
  44.2 0.6 broadcast_subtract_fusion
  44.8 114.0 %all-gather.4.cloned.1.call-done = bf16[3072,6144]{1,0:T(8,128)(2,1)} async-done(((bf16[192,6144]{1,0:T(8,128)(2,1)}), bf16[3072,6144]{1,0:T(8,128)(2,1)}) %all-gather.4.cloned.1.call-update) | async-done | bytes 37748752 | tf_op jit(solution)/shard_map/all_gather | solution.py:10
  158.8 0.0 copy-start
  158.8 89.8 %fusion.3 = (f32[3072]{0:T(1024)S(1)}, f32[3072,2048]{0,1:T(8,128)}) fusion(bf16[3072,6144]{1,0:T(8,128)(2,1)} %all-gather.4.cloned.1.call-done, bf16[6144,2048]{1,0:T(8,128)(2,1)} %param.4), kind=kOutput, calls=%fused_computation.18 | convolution fusion | flops 77315702784 | bytes 88092672 | tf_op jit(solution)/shard_map/dot_general | solution.py:12
  248.7 0.0 copy-done
  248.7 11.7 %exponential_reduce_fusion = (f32[3072]{0:T(1024)S(1)}, f32[3072]{0:T(1024)S(1)}) fusion(f32[3072,2048]{0,1:T(8,128)} %get-tuple-element.16, f32[3072]{0:T(1024)S(1)} %get-tuple-element.15, s32[3072]{0:T(1024)S(1)} %copy-done), kind=kLoop, calls=%fused_computation.5 | loop fusion | flops 31451136 | bytes 25214976 | tf_op jit(solution)/shard_map/reduce_sum | solution.py:15
  260.4 14.2 %all-gather.1 = f32[16,3,3072]{2,1,0:T(4,128)S(1)} all-gather(f32[1,3,3072]{2,1,0:T(4,128)S(1)} %maximum_bitcast_fusion), channel_id=2, replica_groups=mesh['dp'=1,'tp'=16] {'tp'}, dimensions={0}, use_global_device_ids=true | all-gather | bytes 626688 | tf_op jit(solution)/shard_map/all_gather | solution.py:16
  274.6 1.1 slice_reduce_fusion.1
  275.8 0.1 fusion.1
  275.9 89.8 %convolution_convert_fusion = bf16[3072,6144]{1,0:T(8,128)(2,1)} fusion(bf16[6144,2048]{1,0:T(8,128)(2,1)} %param.4, f32[3072,2048]{0,1:T(8,128)} %get-tuple-element.16, f32[3072]{0:T(1024)S(1)} %fusion.1, f32[3072]{0:T(1024)S(1)} %get-tuple-element.11, s32[3072]{0:T(1024)S(1)} %copy-done), kind=kOutput, calls=%fused_computation | convolution fusion | flops 77366034432 | bytes 88117248 | tf_op jit(solution)/shard_map/dot_general | solution.py:22
  365.7 0.0 reduce-scatter.2.cloned.1.call-update
  365.7 126.4 %convert_bitcast_fusion = bf16[6144,2048]{0,1:T(8,128)(2,1)} fusion(bf16[3072,6144]{1,0:T(8,128)(2,1)} %all-gather.4.cloned.1.call-done, f32[3072,2048]{0,1:T(8,128)} %get-tuple-element.16, f32[3072]{0:T(1024)S(1)} %fusion.1, f32[3072]{0:T(1024)S(1)} %get-tuple-element.11, s32[3072]{0:T(1024)S(1)} %copy-done), kind=kOutput, calls=%fused_computation.1 | convolution fusion | flops 77359742976 | bytes 88117248 | tf_op jit(solution)/shard_map/dot_general | solution.py:24
  492.1 32.6 %copy.9 = bf16[6144,2048]{1,0:T(8,128)(2,1)} copy(bf16[6144,2048]{0,1:T(8,128)(2,1)} %convert_bitcast_fusion) | data formatting | bytes 50331648
  524.7 1.3 dynamic-slice_subtract_fusion
  526.0 40.9 %reduce-scatter.2.cloned.1.call-done = bf16[192,6144]{1,0:T(8,128)(2,1)} async-done(((bf16[3072,6144]{1,0:T(8,128)(2,1)}), bf16[192,6144]{1,0:T(8,128)(2,1)}) %reduce-scatter.2.cloned.1.call-update) | async-done | bytes 2359312 | tf_op jit(solution)/shard_map/reduce_scatter | solution.py:23
  (2 shorter events, 0.0 us)
Async XLA Ops:
  7.2 151.6 %all-gather.4.cloned.1.call-start = ((), (), s32[]{:S(2)}) async-start(), calls=%async_computation.1 | async-start | bytes 40108032 | tf_op jit(solution)/shard_map/all_gather | solution.py:10
  7.9 559.0 %reduce-scatter.2.cloned.1.call-start = ((), (), s32[]{:S(2)}) async-start(), calls=%async_computation.2 | async-start | bytes 40108032 | tf_op jit(solution)/shard_map/reduce_scatter | solution.py:23
  158.8 89.8 %copy-start = (s32[3072]{0:T(1024)S(1)}, s32[3072]{0:T(1024)}, u32[]{:S(2)}) copy-start(s32[3072]{0:T(1024)} %broadcast_subtract_fusion) | copy-start | bytes 36868
Sparse Core Ops, SparseCore 0:
  10.2 148.5 all-gather.3
  365.8 201.0 reduce-scatter.1
where the time goes:
time: 575 us; the launch traced here: 574 us
  matrix products  306 us (53%)
  waiting for transfers between devices  156 us (27%)
  blocking collectives  49.6 us (9%)
  local copies, waits for them, and re-layouts  33.5 us (6%)
  other arithmetic  14.9 us (3%)
  between operations  14.1 us (2%)
    dot_general x1, matrix products, step(): jnp.dot(rows.T, by_logits, preferred_element_type=jnp.float32)  126 us
    all_gather x1, waiting for transfers between devices, step(): rows = lax.all_gather(x, 'tp', axis=0, tiled=True)  114 us
    dot_general x1, matrix products, step(): logits = jnp.dot(rows, w, preferred_element_type=jnp.float32)  89.8 us
    dot_general x1, matrix products, step(): jnp.dot(by_logits, w.T, preferred_element_type=jnp.float32)  89.8 us
    reduce_scatter x1, waiting for transfers between devices, step(): by_x = lax.psum_scatter(term, 'tp', scatter_dimension=0, tiled=True)  40.9 us
    unnamed x1, blocking collectives  35.4 us
    unnamed x5, local copies, waits for them, and re-layouts  33.5 us
    all_gather x1, blocking collectives, step(): high, sums, right = jnp.moveaxis(lax.all_gather(own, 'tp'), 1, 0)  14.2 us
  transfers between devices with their start and end apart: 2, of which 2 were waited for; matrix products, arithmetic and copies ran while one was open for 28% of the time, Pallas kernels for 0%

commit v1 on v0

v1 whole, which is shorter than its diff:
```python
import functools

import jax
import jax.numpy as jnp
from jax import lax
from jax.experimental import pallas as pl
from jax.experimental.pallas import tpu as pltpu
from jax.sharding import PartitionSpec as P

F32, BF16 = jnp.float32, jnp.bfloat16
VMEM_LIMIT = 60 * 1024 * 1024
CHUNKS = 4


def dot(a, b, contract):
    return lax.dot_general(a, b, (contract, ((), ())), preferred_element_type=F32)


def exchange_kernel(n, own_ref, all_ref, send_sems, recv_sems):
    me = lax.axis_index("tp")
    barrier = pltpu.get_barrier_semaphore()
    for j in range(1, n):
        pl.semaphore_signal(barrier, inc=1, device_id={"tp": lax.rem(me + j, n)}, device_id_type=pl.DeviceIdType.MESH)
    pl.semaphore_wait(barrier, n - 1)
    copies = []
    for j in range(1, n):
        copy = pltpu.make_async_remote_copy(
            src_ref=own_ref,
            dst_ref=all_ref.at[me],
            send_sem=send_sems.at[j],
            recv_sem=recv_sems.at[j],
            device_id={"tp": lax.rem(me + j, n)},
            device_id_type=pl.DeviceIdType.MESH,
        )
        copy.start()
        copies.append(copy)
    all_ref[me] = own_ref[...]
    for copy in copies:
        copy.wait()


def exchange(own, n, collective_id):
    return pl.pallas_call(
        functools.partial(exchange_kernel, n),
        out_shape=jax.ShapeDtypeStruct((n,) + own.shape, own.dtype),
        in_specs=[pl.BlockSpec(memory_space=pltpu.VMEM)],
        out_specs=pl.BlockSpec(memory_space=pltpu.VMEM),
        scratch_shapes=[pltpu.SemaphoreType.DMA((n,)), pltpu.SemaphoreType.DMA((n,))],
        compiler_params=pltpu.CompilerParams(collective_id=collective_id, has_side_effects=True),
        name="exchange",
    )(own)


def logits_kernel(x_ref, w_ref, lab_ref, z_ref, st_ref, m_s, s_s, r_s):
    j = pl.program_id(0)
    rows, wide = z_ref.shape
    block = 256

    @pl.when(j == 0)
    def _():
        m_s[...] = jnp.full(m_s.shape, -jnp.inf, F32)
        s_s[...] = jnp.zeros(s_s.shape, F32)
        r_s[...] = jnp.zeros(r_s.shape, F32)

    lane = lax.broadcasted_iota(jnp.int32, (block, 128), 1)
    for i in range(0, rows, block):
        part = slice(i, i + block)
        z = dot(x_ref[part, :], w_ref[...], ((1,), (0,)))
        z_ref[part, :] = z
        old = m_s[part, :]
        new = old
        for c in range(0, wide, 128):
            new = jnp.maximum(new, z[:, c : c + 128])
        total = s_s[part, :] * jnp.exp(old - new)
        right = r_s[part, :]
        off = lab_ref[part, :] - j * wide
        for c in range(0, wide, 128):
            total += jnp.exp(z[:, c : c + 128] - new)
            right += jnp.where(lane == off - c, z[:, c : c + 128], 0.0)
        m_s[part, :] = new
        s_s[part, :] = total
        r_s[part, :] = right

    @pl.when(j == pl.num_programs(0) - 1)
    def _():
        high = jnp.max(m_s[...], -1, keepdims=True)
        total = jnp.sum(s_s[...] * jnp.exp(m_s[...] - high), -1, keepdims=True)
        right = jnp.sum(r_s[...], -1, keepdims=True)
        at = lax.broadcasted_iota(jnp.int32, (rows, 128), 1)
        st_ref[...] = jnp.where(at == 0, high, jnp.where(at == 1, total, jnp.where(at == 2, right, 0.0))).T[:8, :]


def logits_call(x, w, lab):
    rows, depth = x.shape
    columns, wide = w.shape[1], 256
    return pl.pallas_call(
        logits_kernel,
        grid=(columns // wide,),
        in_specs=[
            pl.BlockSpec((rows, depth), lambda j: (0, 0)),
            pl.BlockSpec((depth, wide), lambda j: (0, j)),
            pl.BlockSpec((rows, 1), lambda j: (0, 0)),
        ],
        out_specs=[pl.BlockSpec((rows, wide), lambda j: (0, j)), pl.BlockSpec((8, rows), lambda j: (0, 0))],
        out_shape=[jax.ShapeDtypeStruct((rows, columns), F32), jax.ShapeDtypeStruct((8, rows), F32)],
        scratch_shapes=[pltpu.VMEM((rows, 128), F32)] * 3,
        compiler_params=pltpu.CompilerParams(vmem_limit_bytes=VMEM_LIMIT, dimension_semantics=("arbitrary",)),
        cost_estimate=pl.CostEstimate(
            flops=2 * rows * depth * columns, bytes_accessed=2 * depth * (rows + columns) + 4 * rows * columns, transcendentals=0
        ),
        name="logits",
    )(x, w, lab)


def by_x_kernel(z_ref, all_ref, lab_ref, w_ref, term_ref, g_ref, loss_ref, top_s, inv_s):
    j = pl.program_id(0)
    rows, columns = z_ref.shape
    block = 32

    @pl.when(j == 0)
    def _():
        own = all_ref[...]
        high, sums, right = own[:, 0, :], own[:, 1, :], own[:, 2, :]
        top = jnp.max(high, 0, keepdims=True)
        total = jnp.sum(sums * jnp.exp(high - top), 0, keepdims=True)
        loss_ref[...] = jnp.log(total) + top - jnp.sum(right, 0, keepdims=True)
        at = lax.broadcasted_iota(jnp.int32, (128, rows), 0)
        both = jnp.where(at == 0, top, jnp.where(at == 1, 1.0 / total, 0.0)).T
        top_s[...] = jnp.broadcast_to(both[:, 0:1], top_s.shape)
        inv_s[...] = jnp.broadcast_to(both[:, 1:2], inv_s.shape)
        lane = lax.broadcasted_iota(jnp.int32, (block, 128), 1)

        def body(i, carry):
            part = pl.ds(pl.multiple_of(i * block, block), block)
            top_b, inv_b = top_s[part, :], inv_s[part, :]
            off = jnp.broadcast_to(lab_ref[part, :], (block, 128)) - lane
            for c in range(0, columns, 128):
                e = jnp.exp(z_ref[part, c : c + 128] - top_b) * inv_b
                g_ref[part, c : c + 128] = jnp.where(off == c, e - 1.0, e).astype(BF16)
            return carry

        lax.fori_loop(0, rows // block, body, 0)

    term_ref[...] = dot(g_ref[...], w_ref[...], ((1,), (1,))).astype(BF16)


def by_x_call(z, all_stats, lab, w):
    rows, columns = z.shape
    depth, tall = w.shape[0], 512
    n = all_stats.shape[0]
    return pl.pallas_call(
        by_x_kernel,
        grid=(depth // tall,),
        in_specs=[
            pl.BlockSpec((rows, columns), lambda j: (0, 0)),
            pl.BlockSpec((n, 8, rows), lambda j: (0, 0, 0)),
            pl.BlockSpec((rows, 1), lambda j: (0, 0)),
            pl.BlockSpec((tall, columns), lambda j: (j, 0)),
        ],
        out_specs=[
            pl.BlockSpec((rows, tall), lambda j: (0, j)),
            pl.BlockSpec((rows, columns), lambda j: (0, 0)),
            pl.BlockSpec((1, rows), lambda j: (0, 0)),
        ],
        out_shape=[
            jax.ShapeDtypeStruct((rows, depth), BF16),
            jax.ShapeDtypeStruct((rows, columns), BF16),
            jax.ShapeDtypeStruct((1, rows), F32),
        ],
        scratch_shapes=[pltpu.VMEM((rows, 128), F32)] * 2,
        compiler_params=pltpu.CompilerParams(vmem_limit_bytes=VMEM_LIMIT, dimension_semantics=("arbitrary",)),
        cost_estimate=pl.CostEstimate(
            flops=2 * rows * depth * columns, bytes_accessed=2 * depth * (rows + columns) + 6 * rows * columns, transcendentals=0
        ),
        name="by_x",
    )(z, all_stats, lab, w)


def by_w_kernel(k, *refs):
    x_refs, g_refs, out_ref = refs[:k], refs[k : 2 * k], refs[2 * k]
    acc = None
    for x_ref, g_ref in zip(x_refs, g_refs):
        part = dot(x_ref[...], g_ref[...], ((0,), (0,)))
        acc = part if acc is None else acc + part
    out_ref[...] = acc.astype(BF16)


def by_w_call(xs, gs):
    k = len(xs)
    rows, depth = xs[0].shape
    columns, tall = gs[0].shape[1], 256
    return pl.pallas_call(
        functools.partial(by_w_kernel, k),
        grid=(depth // tall,),
        in_specs=[pl.BlockSpec((rows, tall), lambda j: (0, j))] * k + [pl.BlockSpec((rows, columns), lambda j: (0, 0))] * k,
        out_specs=pl.BlockSpec((tall, columns), lambda j: (j, 0)),
        out_shape=jax.ShapeDtypeStruct((depth, columns), BF16),
        compiler_params=pltpu.CompilerParams(vmem_limit_bytes=VMEM_LIMIT, dimension_semantics=("arbitrary",)),
        cost_estimate=pl.CostEstimate(
            flops=2 * k * rows * depth * columns,
            bytes_accessed=2 * k * rows * (depth + columns) + 2 * depth * columns,
            transcendentals=0,
        ),
        name="by_w",
    )(*xs, *gs)


def solution(mesh):
    n = mesh.shape["tp"]

    def step(x, w, label):
        me, own_rows, columns = lax.axis_index("tp"), x.shape[0], w.shape[1]
        r = own_rows // CHUNKS
        xs = [lax.all_gather(x[c * r : (c + 1) * r], "tp", axis=0, tiled=True) for c in range(CHUNKS)]
        padded = jnp.pad(label.reshape(1, own_rows), ((0, 0), (0, -own_rows % 128)))
        wanted = exchange(padded, n, 0)[:, 0, :own_rows].reshape(n, CHUNKS, r) - me * columns
        gs, terms, losses = [], [], []
        for c in range(CHUNKS):
            lab = wanted[:, c, :].reshape(n * r, 1)
            z, own = logits_call(xs[c], w, lab)
            all_stats = exchange(own, n, 1 + c)
            term, g, loss = by_x_call(z, all_stats, lab, w)
            terms.append(lax.psum_scatter(term, "tp", scatter_dimension=0, tiled=True))
            gs.append(g)
            losses.append(lax.dynamic_slice_in_dim(loss, me * r, r, 1)[0])
        by_w = by_w_call(xs, gs)
        return jnp.concatenate(losses), jnp.concatenate(terms), by_w

    return jax.shard_map(
        step,
        mesh=mesh,
        in_specs=(P(("dp", "tp"), None), P(None, "tp"), P(("dp", "tp"))),
        out_specs=(P(("dp", "tp")), P(("dp", "tp"), None), P("dp", "tp")),
        check_vma=False,
    )
```

time: 575 us -> 589 us (1.024)
  Pallas kernels: 0 us -> 382 us
  matrix products: 306 us -> 0 us
  blocking collectives: 49.6 us -> 0 us
  local copies, waits for them, and re-layouts: 33.5 us -> 10.4 us
  waiting for transfers between devices: 156 us -> 174 us
  other arithmetic: 14.9 us -> 4.63 us
    pallas_call x0 -> x14, Pallas kernels: none -> 382 us  [the longest x4 122 us: by_x_call(): pl.pallas_call(by_x_kernel, grid=(depth // tall,), in_specs=[pl.BlockSpec...]
    dot_general x3 -> x0, matrix products: 306 us -> none  [the longest x1 126 us: step(): jnp.dot(rows.T, by_logits, preferred_element_type=jnp.float32)]
    reduce_scatter x1 -> x4, waiting for transfers between devices: 40.9 us -> 130 us  [step(): terms.append(lax.psum_scatter(term, 'tp', scatter_dimension=0, tiled=True))]
    all_gather x1 -> x4, waiting for transfers between devices: 114 us -> 41.9 us  [step(): lax.all_gather(x[c * r:(c + 1) * r], 'tp', axis=0, tiled=True)]
    unnamed x1 -> x0, blocking collectives: 35.4 us -> none
    unnamed x5 -> x2, local copies, waits for them, and re-layouts: 33.5 us -> 0.01 us
    all_gather x1 -> x0, blocking collectives: 14.2 us -> none  [step(): high, sums, right = jnp.moveaxis(lax.all_gather(own, 'tp'), 1, 0)]
    reduce_sum x2 -> x0, other arithmetic: 11.8 us -> none  [the longest x1 11.7 us: step(): jnp.sum(jnp.exp(logits - high[:, None]), -1)]
  transfers between devices with their start and end apart: 2 -> 8, of which waited for: 2 -> 3; matrix products, arithmetic and copies ran while one was open for 28% -> 1% of each run, Pallas kernels for 0% -> 65%
where the time goes in v1:
time: 589 us; the launch traced here: 586 us
  Pallas kernels  382 us (65%)
  waiting for transfers between devices  174 us (30%)
  between operations  14.2 us (2%)
  local copies, waits for them, and re-layouts  10.4 us (2%)
    reduce_scatter x4, waiting for transfers between devices, step(): terms.append(lax.psum_scatter(term, 'tp', scatter_dimension=0, tiled=True))  130 us
    pallas_call x4, Pallas kernels, by_x_call(): pl.pallas_call(by_x_kernel, grid=(depth // tall,), in_specs=[pl.BlockSpec...  122 us
    pallas_call x4, Pallas kernels, logits_call(): pl.pallas_call(logits_kernel, grid=(columns // wide,), in_specs=[pl.Block...  114 us
    pallas_call x1, Pallas kernels, by_w_call(): pl.pallas_call(functools.partial(by_w_kernel, k), grid=(depth // tall,),...  89.9 us
    pallas_call x5, Pallas kernels, exchange(): pl.pallas_call(functools.partial(exchange_kernel, n), out_shape=jax.Shape...  55.9 us
    all_gather x4, waiting for transfers between devices, step(): lax.all_gather(x[c * r:(c + 1) * r], 'tp', axis=0, tiled=True)  41.9 us
  transfers between devices with their start and end apart: 8, of which 3 were waited for; matrix products, arithmetic and copies ran while one was open for 1% of the time, Pallas kernels for 65%

profile of v1, /device:TPU:0, one launch (start us, length us, event | category | flops | bytes accessed | tf_op | source)
XLA Modules:
  0.0 586.2 jit_solution(11228576557149279096)
XLA Ops:
  7.2 3.0 fusion.4
  10.3 0.7 all-gather.11.cloned.1.call-update
  11.1 0.7 all-gather.7.cloned.1.call-update
  12.4 0.6 pad.4.own_ref
  13.0 8.9 %exchange.5 = s32[16,1,256]{2,1,0:T(1,128)} custom-call(s32[1,256]{1,0:T(1,128)} %pad.4.own_ref), custom_call_target="tpu_custom_call" | custom-call | tf_op jit(solution)/shard_map/exchange/pallas_call | solution.py:43
  21.9 0.8 subtract_reduce_fusion
  22.8 0.9 reshape_squeeze.19.lab_ref
  23.8 41.9 %all-gather.9.cloned.1.call-done.x_ref.refs_2_ = bf16[768,6144]{1,0:T(8,128)(2,1)} async-done(((bf16[48,6144]{1,0:T(8,128)(2,1)}), bf16[768,6144]{1,0:T(8,128)(2,1)}) %all-gather.9.cloned.1.call-update) | async-done | bytes 9437200 | tf_op jit(solution)/shard_map/all_gather | solution.py:214
  65.7 28.8 %logits.6 = (f32[768,2048]{1,0:T(8,128)}, f32[8,768]{1,0:T(8,128)}) custom-call(bf16[768,6144]{1,0:T(8,128)(2,1)} %all-gather.9.cloned.1.call-done.x_ref.refs_2_, bf16[6144,2048]{1,0:T(8,128)(2,1)} %w_ref.15, s32[768,1]{1,0:T(8,128)} %reshape_squeeze.19.lab_ref), custom_call_target="tpu_custom_call" | custom-call | flops 19327352832 | bytes 40894464 | tf_op jit(solution)/shard_map/logits/pallas_call | solution.py:96
  94.4 12.6 %exchange.8.all_ref = f32[16,8,768]{2,1,0:T(8,128)} custom-call(f32[8,768]{1,0:T(8,128)} %get-tuple-element.30.own_ref), custom_call_target="tpu_custom_call" | custom-call | tf_op jit(solution)/shard_map/exchange/pallas_call | solution.py:43
  107.0 30.5 %by_x.6 = (bf16[768,6144]{1,0:T(8,128)(2,1)}, bf16[768,2048]{1,0:T(8,128)(2,1)}, f32[1,768]{1,0:T(1,128)}) custom-call(f32[768,2048]{1,0:T(8,128)} %get-tuple-element.29.z_ref, f32[16,8,768]{2,1,0:T(8,128)} %exchange.8.all_ref, s32[768,1]{1,0:T(8,128)} %reshape_squeeze.19.lab_ref, bf16[6144,2048]{1,0:T(8,128)(2,1)} %w_ref.15), custom_call_target="tpu_custom_call" | custom-call | flops 19327352832 | bytes 44040192 | tf_op jit(solution)/shard_map/by_x/pallas_call | solution.py:151
  137.6 0.9 reshape_squeeze.20.lab_ref
  138.5 28.6 %logits.7 = (f32[768,2048]{1,0:T(8,128)}, f32[8,768]{1,0:T(8,128)}) custom-call(bf16[768,6144]{1,0:T(8,128)(2,1)} %all-gather.11.cloned.1.call-done.x_ref.refs_3_, bf16[6144,2048]{1,0:T(8,128)(2,1)} %w_ref.15, s32[768,1]{1,0:T(8,128)} %reshape_squeeze.20.lab_ref), custom_call_target="tpu_custom_call" | custom-call | flops 19327352832 | bytes 40894464 | tf_op jit(solution)/shard_map/logits/pallas_call | solution.py:96
  167.1 11.2 %exchange.9.all_ref = f32[16,8,768]{2,1,0:T(8,128)} custom-call(f32[8,768]{1,0:T(8,128)} %get-tuple-element.33.own_ref), custom_call_target="tpu_custom_call" | custom-call | tf_op jit(solution)/shard_map/exchange/pallas_call | solution.py:43
  178.3 30.6 %by_x.7 = (bf16[768,6144]{1,0:T(8,128)(2,1)}, bf16[768,2048]{1,0:T(8,128)(2,1)}, f32[1,768]{1,0:T(1,128)}) custom-call(f32[768,2048]{1,0:T(8,128)} %get-tuple-element.32.z_ref, f32[16,8,768]{2,1,0:T(8,128)} %exchange.9.all_ref, s32[768,1]{1,0:T(8,128)} %reshape_squeeze.20.lab_ref, bf16[6144,2048]{1,0:T(8,128)(2,1)} %w_ref.15), custom_call_target="tpu_custom_call" | custom-call | flops 19327352832 | bytes 44040192 | tf_op jit(solution)/shard_map/by_x/pallas_call | solution.py:151
  209.1 0.9 reshape_squeeze.18.lab_ref
  210.1 28.6 %logits.5 = (f32[768,2048]{1,0:T(8,128)}, f32[8,768]{1,0:T(8,128)}) custom-call(bf16[768,6144]{1,0:T(8,128)(2,1)} %all-gather.7.cloned.1.call-done.x_ref.refs_1_, bf16[6144,2048]{1,0:T(8,128)(2,1)} %w_ref.15, s32[768,1]{1,0:T(8,128)} %reshape_squeeze.18.lab_ref), custom_call_target="tpu_custom_call" | custom-call | flops 19327352832 | bytes 40894464 | tf_op jit(solution)/shard_map/logits/pallas_call | solution.py:96
  238.7 11.1 %exchange.7.all_ref = f32[16,8,768]{2,1,0:T(8,128)} custom-call(f32[8,768]{1,0:T(8,128)} %get-tuple-element.27.own_ref), custom_call_target="tpu_custom_call" | custom-call | tf_op jit(solution)/shard_map/exchange/pallas_call | solution.py:43
  249.8 30.5 %by_x.5 = (bf16[768,6144]{1,0:T(8,128)(2,1)}, bf16[768,2048]{1,0:T(8,128)(2,1)}, f32[1,768]{1,0:T(1,128)}) custom-call(f32[768,2048]{1,0:T(8,128)} %get-tuple-element.26.z_ref, f32[16,8,768]{2,1,0:T(8,128)} %exchange.7.all_ref, s32[768,1]{1,0:T(8,128)} %reshape_squeeze.18.lab_ref, bf16[6144,2048]{1,0:T(8,128)(2,1)} %w_ref.15), custom_call_target="tpu_custom_call" | custom-call | flops 19327352832 | bytes 44040192 | tf_op jit(solution)/shard_map/by_x/pallas_call | solution.py:151
  280.3 0.9 reshape_squeeze.17.lab_ref
  281.3 28.5 %logits.4 = (f32[768,2048]{1,0:T(8,128)}, f32[8,768]{1,0:T(8,128)}) custom-call(bf16[768,6144]{1,0:T(8,128)(2,1)} %all-gather.5.cloned.1.call-done.x_ref.refs_0_, bf16[6144,2048]{1,0:T(8,128)(2,1)} %w_ref.15, s32[768,1]{1,0:T(8,128)} %reshape_squeeze.17.lab_ref), custom_call_target="tpu_custom_call" | custom-call | flops 19327352832 | bytes 40894464 | tf_op jit(solution)/shard_map/logits/pallas_call | solution.py:96
  309.8 12.0 %exchange.6.all_ref = f32[16,8,768]{2,1,0:T(8,128)} custom-call(f32[8,768]{1,0:T(8,128)} %get-tuple-element.24.own_ref), custom_call_target="tpu_custom_call" | custom-call | tf_op jit(solution)/shard_map/exchange/pallas_call | solution.py:43
  321.8 30.5 %by_x.4 = (bf16[768,6144]{1,0:T(8,128)(2,1)}, bf16[768,2048]{1,0:T(8,128)(2,1)}, f32[1,768]{1,0:T(1,128)}) custom-call(f32[768,2048]{1,0:T(8,128)} %get-tuple-element.23.z_ref, f32[16,8,768]{2,1,0:T(8,128)} %exchange.6.all_ref, s32[768,1]{1,0:T(8,128)} %reshape_squeeze.17.lab_ref, bf16[6144,2048]{1,0:T(8,128)(2,1)} %w_ref.15), custom_call_target="tpu_custom_call" | custom-call | flops 19327352832 | bytes 44040192 | tf_op jit(solution)/shard_map/by_x/pallas_call | solution.py:151
  352.3 0.8 fusion.2
  353.0 0.7 fusion.3
  353.7 0.8 fusion.1
  354.5 0.8 fusion
  355.2 0.6 pad_maximum_fusion.1
  355.9 89.9 %by_w.1 = bf16[6144,2048]{1,0:T(8,128)(2,1)} custom-call(bf16[768,6144]{1,0:T(8,128)(2,1)} %all-gather.5.cloned.1.call-done.x_ref.refs_0_, bf16[768,6144]{1,0:T(8,128)(2,1)} %all-gather.7.cloned.1.call-done.x_ref.refs_1_, bf16[768,6144]{1,0:T(8,128)(2,1)} %all-gather.9.cloned.1.call-done.x_ref.refs_2_, ...), custom_call_target="tpu_custom_call" | custom-call | flops 77309411328 | bytes 75497472 | tf_op jit(solution)/shard_map/by_w/pallas_call | solution.py:192
  445.8 46.2 %reduce-scatter.7.cloned.1.call-done = bf16[48,6144]{1,0:T(8,128)(2,1)} async-done(((bf16[768,6144]{1,0:T(8,128)(2,1)}), bf16[48,6144]{1,0:T(8,128)(2,1)}) %reduce-scatter.7.cloned.1.call-update) | async-done | bytes 589840 | tf_op jit(solution)/shard_map/reduce_scatter | solution.py:223
  492.0 84.1 %reduce-scatter.5.cloned.1.call-done = bf16[48,6144]{1,0:T(8,128)(2,1)} async-done(((bf16[768,6144]{1,0:T(8,128)(2,1)}), bf16[48,6144]{1,0:T(8,128)(2,1)}) %reduce-scatter.5.cloned.1.call-update) | async-done | bytes 589840 | tf_op jit(solution)/shard_map/reduce_scatter | solution.py:223
  576.1 3.2 pad_maximum_fusion
  (23 shorter events, 1.2 us)
Async XLA Ops:
  7.2 5.2 copy-start
  7.2 58.5 %all-gather.9.cloned.1.call-start = ((), (), s32[]{:S(2)}) async-start(), calls=%async_computation.6 | async-start | bytes 10027008 | tf_op jit(solution)/shard_map/all_gather | solution.py:214
  10.3 128.2 %all-gather.11.cloned.1.call-start = ((), (), s32[]{:S(2)}) async-start(), calls=%async_computation.7 | async-start | bytes 10027008 | tf_op jit(solution)/shard_map/all_gather | solution.py:214
  11.0 199.0 %all-gather.7.cloned.1.call-start = ((), (), s32[]{:S(2)}) async-start(), calls=%async_computation.5 | async-start | bytes 10027008 | tf_op jit(solution)/shard_map/all_gather | solution.py:214
  11.8 269.5 %all-gather.5.cloned.1.call-start = ((), (), s32[]{:S(2)}) async-start(), calls=%async_computation.4 | async-start | bytes 10027008 | tf_op jit(solution)/shard_map/all_gather | solution.py:214
  12.3 433.4 %reduce-scatter.9.cloned.1.call-start = ((), (), s32[]{:S(2)}) async-start(), calls=%async_computation.10 | async-start | bytes 10027008 | tf_op jit(solution)/shard_map/reduce_scatter | solution.py:223
  137.6 308.2 %reduce-scatter.11.cloned.1.call-start = ((), (), s32[]{:S(2)}) async-start(), calls=%async_computation.11 | async-start | bytes 10027008 | tf_op jit(solution)/shard_map/reduce_scatter | solution.py:223
  208.9 283.1 %reduce-scatter.7.cloned.1.call-start = ((), (), s32[]{:S(2)}) async-start(), calls=%async_computation.9 | async-start | bytes 10027008 | tf_op jit(solution)/shard_map/reduce_scatter | solution.py:223
  280.3 295.8 %reduce-scatter.5.cloned.1.call-start = ((), (), s32[]{:S(2)}) async-start(), calls=%async_computation.8 | async-start | bytes 10027008 | tf_op jit(solution)/shard_map/reduce_scatter | solution.py:223
Sparse Core Ops, SparseCore 0:
  10.8 54.8 all-gather.8
  67.9 54.6 all-gather.10
  124.8 55.9 all-gather.6
  183.5 52.0 all-gather.4
  240.2 83.5 reduce-scatter.8
  328.4 79.4 reduce-scatter.10
  412.5 79.4 reduce-scatter.6
  496.7 79.4 reduce-scatter.4

commit v2 on v0

v2 whole, which is shorter than its diff:
```python
import functools

import jax
import jax.numpy as jnp
from jax import lax
from jax.experimental import pallas as pl
from jax.experimental.pallas import tpu as pltpu
from jax.sharding import PartitionSpec as P

F32, BF16 = jnp.float32, jnp.bfloat16
MESH = pl.DeviceIdType.MESH
VMEM_LIMIT = 63 * 1024 * 1024

ORDERS = ((4, 2, 1), (2, 1, 4), (1, 4, 2))
MASKS = tuple((0, a, b, c, a | b, a | c, b | c, a | b | c) for a, b, c in ORDERS)
LAST = (None, 0, 1, 2, 1, 2, 2, 2)
BEFORE = (None, 0, 0, 0, 1, 1, 2, 4)
BATCHES, PIECES = 8, 3
BY_W_TALL = 256
BY_W_EARLY = 10


def dot(a, b, contract):
    return lax.dot_general(a, b, (contract, ((), ())), preferred_element_type=F32)


def flip(index, mask):
    for bit in (1, 2, 4, 8):
        if mask & bit:
            index = index + bit - 2 * bit * lax.rem(lax.div(index, bit), 2)
    return index


def across(me, i, k):
    return {"tp": flip(me, 2 * ORDERS[i][LAST[k]])}


def meet(n, me):
    barrier = pltpu.get_barrier_semaphore()
    for j in range(1, n):
        pl.semaphore_signal(barrier, inc=1, device_id={"tp": lax.rem(me + j, n)}, device_id_type=MESH)
    pl.semaphore_wait(barrier, n - 1)


def to_all(n, me, own_ref, all_ref, send_sems, recv_sems):
    copies = []
    for j in range(1, n):
        copies.append(
            pltpu.make_async_remote_copy(
                src_ref=own_ref,
                dst_ref=all_ref.at[me],
                send_sem=send_sems.at[j],
                recv_sem=recv_sems.at[j],
                device_id={"tp": lax.rem(me + j, n)},
                device_id_type=MESH,
            )
        )
    for copy in copies:
        copy.start()
    return copies


def as_column(row):
    return jnp.broadcast_to(row, (128, 128)).T


def logits_kernel(
    n, x_ref, w_ref, lab_ref, xb_ref, z_ref, labs_ref, top_ref, inv_ref, loss_ref,
    w_v, x_v, z_v, m_s, s_s, r_s, off_s, st_s, own_s, all_s,
    w_sem, x_sem, keep_sem, z_sem, ici_send, ici_recv, pair_send, pair_recv, lab_send, lab_recv, st_send, st_recv,
):
    me = lax.axis_index("tp")
    core = lax.rem(me, 2)
    piece = x_ref.shape[0] // PIECES
    half = PIECES * piece
    depth, columns = w_ref.shape
    wide = 256

    w_parts = 8
    w_copies = []
    for p in range(w_parts):
        part = pl.ds(p * (depth // w_parts), depth // w_parts)
        w_copies.append(pltpu.make_async_copy(w_ref.at[part], w_v.at[part], w_sem.at[p]))
        w_copies[-1].start()
    x_load = pltpu.make_async_copy(x_ref, x_v.at[0], x_sem.at[0, 0])
    x_load.start()

    meet(n, me)

    def slot(k, i, other):
        return xb_ref.at[k, pl.ds(i * 2 * piece + other * piece, piece)]

    def source(k, i):
        return x_ref.at[pl.ds(i * piece, piece)] if k == 0 else slot(k, i, 0)

    sent = {}

    def send(k, i):
        sent["ici", k, i] = pltpu.make_async_remote_copy(
            src_ref=source(BEFORE[k], i),
            dst_ref=slot(k, i, 0),
            send_sem=ici_send.at[k, i],
            recv_sem=ici_recv.at[k, i],
            device_id=across(me, i, k),
            device_id_type=MESH,
        )
        sent["ici", k, i].start()

    def share(k, i):
        sent["pair", k, i] = pltpu.make_async_remote_copy(
            src_ref=source(k, i),
            dst_ref=slot(k, i, 1),
            send_sem=pair_send.at[k, i],
            recv_sem=pair_recv.at[k, i],
            device_id={"tp": flip(me, 1)},
            device_id_type=MESH,
        )
        sent["pair", k, i].start()

    labels = to_all(n, me, lab_ref, labs_ref, lab_send, lab_recv)
    for i in range(PIECES):
        send(1, i)
    for i in range(PIECES):
        share(0, i)
    for k in (2, 3):
        for i in range(PIECES):
            send(k, i)
    labs_ref[me] = lab_ref[...]
    x_load.wait()
    kept = []
    for i in range(PIECES):
        kept.append(pltpu.make_async_copy(x_v.at[0, pl.ds(i * piece, piece)], slot(0, i, 0), keep_sem.at[i]))
        kept[-1].start()
    for copy in labels:
        copy.wait_recv()
    for copy in w_copies:
        copy.wait()

    z_copies = {0: [], 1: []}
    lane = lax.broadcasted_iota(jnp.int32, (half, 128), 1)

    def compute(k, other):
        for i in range(PIECES):
            dev = flip(me, 2 * MASKS[i][k] + other)
            row = (labs_ref[dev, pl.ds(i, 1), :] - me * columns).astype(F32)
            off_s[pl.ds(i * piece, piece), :] = as_column(row)[:piece].astype(jnp.int32)
        m_s[...] = jnp.full(m_s.shape, -jnp.inf, F32)
        s_s[...] = jnp.zeros(s_s.shape, F32)
        r_s[...] = jnp.zeros(r_s.shape, F32)
        for copy in z_copies[other]:
            copy.wait()

        def body(j, carry):
            at = pl.multiple_of(j * wide, wide)
            z = dot(x_v[other], w_v[:, pl.ds(at, wide)], ((1,), (0,)))
            z_v[other, :, pl.ds(at, wide)] = z
            old = m_s[...]
            new = old
            for c in range(0, wide, 128):
                new = jnp.maximum(new, z[:, c : c + 128])
            total = s_s[...] * jnp.exp(old - new)
            right = r_s[...]
            off = off_s[...] - at
            for c in range(0, wide, 128):
                total += jnp.exp(z[:, c : c + 128] - new)
                right += jnp.where(lane == off - c, z[:, c : c + 128], 0.0)
            m_s[...] = new
            s_s[...] = total
            r_s[...] = right
            return carry

        lax.fori_loop(0, columns // wide, body, 0)
        z_copies[other] = []
        for i in range(PIECES):
            z_copies[other].append(
                pltpu.make_async_copy(
                    z_v.at[other, pl.ds(i * piece, piece)],
                    z_ref.at[k, pl.ds(i * 2 * piece + other * piece, piece)],
                    z_sem.at[other, i],
                )
            )
            z_copies[other][-1].start()
        high = jnp.max(m_s[...], -1, keepdims=True)
        total = jnp.sum(s_s[...] * jnp.exp(m_s[...] - high), -1, keepdims=True)
        right = jnp.sum(r_s[...], -1, keepdims=True)
        st_s[other] = jnp.where(lane == 0, high, jnp.where(lane == 1, total, jnp.where(lane == 2, right, 0.0)))

    def load(k, other):
        copies = []
        for i in range(PIECES):
            copies.append(pltpu.make_async_copy(slot(k, i, other), x_v.at[other, pl.ds(i * piece, piece)], x_sem.at[other, i]))
            copies[-1].start()
        return copies

    for k in range(BATCHES):
        if k > 0:
            for i in range(PIECES):
                sent["ici", k, i].wait_recv()
            for i in range(PIECES):
                for later in range(4, BATCHES):
                    if BEFORE[later] == k:
                        send(later, i)
                share(k, i)
            for copy in load(k, 0):
                copy.wait()
        compute(k, 0)
        for i in range(PIECES):
            sent["pair", k, i].wait_recv()
        if k == 0:
            for copy in kept:
                copy.wait()
        for copy in load(k, 1):
            copy.wait()
        compute(k, 1)
        for i in range(PIECES):
            part = pl.ds(i * piece, piece)
            first, second = st_s[0, part, :], st_s[1, part, :]
            both = jnp.concatenate(
                [jnp.where(core == 0, first, second), jnp.where(core == 0, second, first)], 0
            ).T
            pair = lax.div(flip(me, 2 * MASKS[i][k]), 2) * PIECES + i
            for t in range(3):
                own_s[t, pl.ds(pair, 1), :] = both[t : t + 1, :]

    stats = to_all(n, me, own_s, all_s, st_send, st_recv)
    all_s[me] = own_s[...]
    for copy in stats:
        copy.wait_recv()
    high, sums, right = all_s[:, 0], all_s[:, 1], all_s[:, 2]
    top = jnp.max(high, 0)
    total = jnp.sum(sums * jnp.exp(high - top[None]), 0)
    top_ref[...] = top
    inv_ref[...] = 1.0 / total
    loss_ref[...] = jnp.log(total) + top - jnp.sum(right, 0)
    for copy in labels + stats + list(sent.values()):
        copy.wait_send()
    for copies in z_copies.values():
        for copy in copies:
            copy.wait()


def logits_call(n, x, w, lab):
    own, depth = x.shape
    columns = w.shape[1]
    pairs = n // 2 * PIECES
    anywhere, vmem = pl.BlockSpec(memory_space=pl.ANY), pl.BlockSpec(memory_space=pltpu.VMEM)
    dma = pltpu.SemaphoreType.DMA
    return pl.pallas_call(
        functools.partial(logits_kernel, n),
        in_specs=[anywhere, anywhere, vmem],
        out_specs=[anywhere, anywhere, vmem, vmem, vmem, vmem],
        out_shape=[
            jax.ShapeDtypeStruct((BATCHES, 2 * own, depth), BF16),
            jax.ShapeDtypeStruct((BATCHES, 2 * own, columns), F32),
            jax.ShapeDtypeStruct((n,) + lab.shape, jnp.int32),
            jax.ShapeDtypeStruct((pairs, 128), F32),
            jax.ShapeDtypeStruct((pairs, 128), F32),
            jax.ShapeDtypeStruct((pairs, 128), F32),
        ],
        scratch_shapes=[
            pltpu.VMEM((depth, columns), BF16),
            pltpu.VMEM((2, own, depth), BF16),
            pltpu.VMEM((2, own, columns), F32),
            pltpu.VMEM((own, 128), F32),
            pltpu.VMEM((own, 128), F32),
            pltpu.VMEM((own, 128), F32),
            pltpu.VMEM((own, 128), jnp.int32),
            pltpu.VMEM((2, own, 128), F32),
            pltpu.VMEM((3, pairs, 128), F32),
            pltpu.VMEM((n, 3, pairs, 128), F32),
            dma((8,)),
            dma((2, PIECES)),
            dma((PIECES,)),
            dma((2, PIECES)),
            dma((BATCHES, PIECES)),
            dma((BATCHES, PIECES)),
            dma((BATCHES, PIECES)),
            dma((BATCHES, PIECES)),
            dma((n,)),
            dma((n,)),
            dma((n,)),
            dma((n,)),
        ],
        compiler_params=pltpu.CompilerParams(vmem_limit_bytes=VMEM_LIMIT, collective_id=0, has_side_effects=True),
        cost_estimate=pl.CostEstimate(flops=2 * n * own * depth * columns, bytes_accessed=1 << 27, transcendentals=0),
        name="gather_logits",
    )(x, w, lab)


PASSES = (((7,), ()), ((6, 5), (7,)), ((4, 3), (6, 5)), ((2, 1), (4, 3)), ((0,), (2, 1)), ((), (0,)))


def joins(k):
    return tuple(b for b in range(1, BATCHES) if BEFORE[b] == k)


def scatter_kernel(
    n, z_ref, w_ref, x_ref, top_ref, inv_ref, lab_ref,
    out_ref, g_ref, part_ref, give_ref, took_ref, pass_ref, came_ref, last_ref,
    z_v, g_v, top_s, inv_s, off_s, gw_v, z_sem, g_sem, gw_sem, pair_send, pair_recv, ici_send, ici_recv,
):
    me = lax.axis_index("tp")
    core = lax.rem(me, 2)
    half = z_ref.shape[1] // 2
    piece = half // PIECES
    depth, columns = w_ref.shape
    wide = 512

    groups = [[(k, 1) for k in given] + [(k, 0) for k in own] for given, own in PASSES]
    flat = [group for one in groups for group in one]

    def load(number):
        k, other = flat[number]
        return [
            pltpu.make_async_copy(
                z_ref.at[k, pl.ds(i * 2 * piece + other * piece, piece)],
                z_v.at[number % 2, pl.ds(i * piece, piece)],
                z_sem.at[number % 2, i],
            )
            for i in range(PIECES)
        ]

    def start(copies):
        for copy in copies:
            copy.start()
        return copies

    loading = start(load(0))
    meet(n, me)

    lane = lax.broadcasted_iota(jnp.int32, (32, 128), 1)
    sent = {}
    number = 0
    for given, own in PASSES:
        rows = half * (len(given) + len(own))
        g_copies = []
        for place, (k, other) in enumerate([(k, 1) for k in given] + [(k, 0) for k in own]):
            for i in range(PIECES):
                pair = lax.div(flip(me, 2 * MASKS[i][k]), 2) * PIECES + i
                for from_ref, to_ref in ((top_ref, top_s), (inv_ref, inv_s), (lab_ref, off_s)):
                    both = as_column(from_ref[pl.ds(pair, 1), :])
                    to_ref[pl.ds(i * piece, piece), :] = jnp.where(core == other, both[:piece], both[piece:])
            for copy in loading:
                copy.wait()
            slot = number % 2
            number += 1
            if number < len(flat):
                loading = start(load(number))

            def body(b, carry, slot=slot, place=place):
                part = pl.ds(pl.multiple_of(b * 32, 32), 32)
                to = pl.ds(pl.multiple_of(place * half + b * 32, 32), 32)
                top, inv, off = top_s[part, :], inv_s[part, :], off_s[part, :].astype(jnp.int32) - lane
                for c in range(0, columns, 128):
                    e = jnp.exp(z_v[slot, part, c : c + 128] - top) * inv
                    g_v[to, c : c + 128] = jnp.where(off == c, e - 1.0, e).astype(BF16)
                return carry

            lax.fori_loop(0, half // 32, body, 0)
            for i in range(PIECES):
                g_copies.append(
                    pltpu.make_async_copy(
                        g_v.at[pl.ds(place * half + i * piece, piece)],
                        g_ref.at[k, pl.ds(i * 2 * piece + other * piece, piece)],
                        g_sem.at[place, i],
                    )
                )
                g_copies[-1].start()

        arrivals = []
        for k in own:
            sent["pair", k].wait_recv()
            arrivals.append(took_ref.at[k])
            if k > 0:
                for b in joins(k):
                    for i in range(PIECES):
                        sent["ici", b, i].wait_recv()
                    arrivals.append(came_ref.at[b])
        results = [give_ref.at[k] for k in given] + [pass_ref.at[k] if k > 0 else last_ref for k in own]

        def multiply(*refs, given=given, own=own, rows=rows):
            w_tile, refs = refs[0], list(refs[1:])
            term = dot(g_v[:rows, :], w_tile[...], ((1,), (1,)))
            place = 0
            taken = len(own) + sum(len(joins(k)) for k in own if k > 0)
            ins, outs = refs[:taken], refs[taken:]
            for _ in given:
                outs.pop(0)[...] = term[place : place + half].astype(BF16)
                place += half
            for k in own:
                value = term[place : place + half]
                for _ in range(1 + (len(joins(k)) if k > 0 else 0)):
                    value = value + ins.pop(0)[...].astype(F32)
                out = outs.pop(0)
                out[...] = value.astype(out.dtype)
                place += half

        tile = pl.BlockSpec((half, wide), lambda j: (0, j))
        pltpu.emit_pipeline(
            multiply,
            grid=(depth // wide,),
            in_specs=[pl.BlockSpec((wide, columns), lambda j: (j, 0))] + [tile] * len(arrivals),
            out_specs=[tile] * len(results),
        )(w_ref, *arrivals, *results)
        for copy in g_copies:
            copy.wait()
        for k in own:
            if k > 0:
                for i in range(PIECES):
                    part = pl.ds(i * piece, piece)
                    sent["ici", k, i] = pltpu.make_async_remote_copy(
                        src_ref=pass_ref.at[k, part],
                        dst_ref=came_ref.at[k, part],
                        send_sem=ici_send.at[k, i],
                        recv_sem=ici_recv.at[k, i],
                        device_id=across(me, i, k),
                        device_id_type=MESH,
                    )
                    sent["ici", k, i].start()
        for k in given:
            sent["pair", k] = pltpu.make_async_remote_copy(
                src_ref=give_ref.at[k],
                dst_ref=took_ref.at[k],
                send_sem=pair_send.at[k],
                recv_sem=pair_recv.at[k],
                device_id={"tp": flip(me, 1)},
                device_id_type=MESH,
            )
            sent["pair", k].start()

    load_g = [
        pltpu.make_async_copy(g_ref.at[k], gw_v.at[pl.ds(k * 2 * half, 2 * half)], gw_sem.at[k]) for k in range(BATCHES)
    ]
    for copy in start(load_g):
        copy.wait()

    def outer(x_tile, out_tile):
        out_tile[...] = dot(x_tile[...], gw_v[...], ((0,), (0,))).astype(BF16)

    pltpu.emit_pipeline(
        outer,
        grid=(part_ref.shape[0] // BY_W_TALL,),
        in_specs=[pl.BlockSpec((BATCHES * 2 * half, BY_W_TALL), lambda j: (0, j))],
        out_specs=[pl.BlockSpec((BY_W_TALL, columns), lambda j: (j, 0))],
    )(x_ref, part_ref)

    for b in joins(0):
        for i in range(PIECES):
            sent["ici", b, i].wait_recv()

    def finish(last, *refs):
        value = last[...]
        for ref in refs[:-1]:
            value = value + ref[...].astype(F32)
        refs[-1][...] = value.astype(BF16)

    tile = pl.BlockSpec((half, 1024), lambda j: (0, j))
    pltpu.emit_pipeline(
        finish, grid=(depth // 1024,), in_specs=[tile] * (1 + len(joins(0))), out_specs=[tile]
    )(last_ref, *[came_ref.at[b] for b in joins(0)], out_ref)
    for copy in sent.values():
        copy.wait_send()


def scatter_call(n, z, w, xb, top, inv, lab):
    depth, columns = w.shape
    half = z.shape[1] // 2
    anywhere, vmem = pl.BlockSpec(memory_space=pl.ANY), pl.BlockSpec(memory_space=pltpu.VMEM)
    dma = pltpu.SemaphoreType.DMA
    moved = jax.ShapeDtypeStruct((BATCHES, half, depth), BF16)
    most = max(len(given) + len(own) for given, own in PASSES)
    return pl.pallas_call(
        functools.partial(scatter_kernel, n),
        in_specs=[anywhere, anywhere, anywhere, vmem, vmem, vmem],
        out_specs=[anywhere] * 8,
        out_shape=[
            jax.ShapeDtypeStruct((half, depth), BF16),
            jax.ShapeDtypeStruct(z.shape, BF16),
            jax.ShapeDtypeStruct((BY_W_EARLY * BY_W_TALL, columns), BF16),
            moved,
            moved,
            moved,
            moved,
            jax.ShapeDtypeStruct((half, depth), F32),
        ],
        scratch_shapes=[
            pltpu.VMEM((2, half, columns), F32),
            pltpu.VMEM((most * half, columns), BF16),
            pltpu.VMEM((half, 128), F32),
            pltpu.VMEM((half, 128), F32),
            pltpu.VMEM((half, 128), F32),
            pltpu.VMEM((BATCHES * 2 * half, columns), BF16),
            dma((2, PIECES)),
            dma((most, PIECES)),
            dma((BATCHES,)),
            dma((BATCHES,)),
            dma((BATCHES,)),
            dma((BATCHES, PIECES)),
            dma((BATCHES, PIECES)),
        ],
        compiler_params=pltpu.CompilerParams(vmem_limit_bytes=VMEM_LIMIT, collective_id=1, has_side_effects=True),
        cost_estimate=pl.CostEstimate(flops=3 * n * half * depth * columns, bytes_accessed=1 << 28, transcendentals=0),
        name="by_x_scatter",
    )(z, w, xb, top, inv, lab)


def by_w_kernel(x_ref, g_ref, part_ref, out_ref, g_v, part_v, g_sem, part_sem):
    rows, columns = g_ref.shape
    early = part_ref.shape[0]
    g_load = [
        pltpu.make_async_copy(g_ref.at[pl.ds(p * rows // 8, rows // 8)], g_v.at[pl.ds(p * rows // 8, rows // 8)], g_sem.at[p])
        for p in range(8)
    ]
    load = pltpu.make_async_copy(part_ref, part_v, part_sem.at[0])
    for copy in g_load:
        copy.start()
    load.start()
    for copy in g_load:
        copy.wait()

    def outer(x_tile, out_tile):
        out_tile[...] = dot(x_tile[...], g_v[...], ((0,), (0,))).astype(BF16)

    tiles = (out_ref.shape[0] - early) // BY_W_TALL

    def run(first, count):
        skip = early // BY_W_TALL + first
        pltpu.emit_pipeline(
            outer,
            grid=(count,),
            in_specs=[pl.BlockSpec((rows, BY_W_TALL), lambda j: (0, skip + j))],
            out_specs=[pl.BlockSpec((BY_W_TALL, columns), lambda j: (skip + j, 0))],
        )(x_ref, out_ref)

    run(0, tiles // 2)
    load.wait()
    store = pltpu.make_async_copy(part_v, out_ref.at[pl.ds(0, early)], part_sem.at[1])
    store.start()
    run(tiles // 2, tiles - tiles // 2)
    store.wait()


def by_w_call(xb, g, part):
    rows, depth = xb.shape
    columns = g.shape[1]
    anywhere = pl.BlockSpec(memory_space=pl.ANY)
    dma = pltpu.SemaphoreType.DMA
    return pl.pallas_call(
        by_w_kernel,
        in_specs=[anywhere] * 3,
        out_specs=anywhere,
        out_shape=jax.ShapeDtypeStruct((depth, columns), BF16),
        scratch_shapes=[pltpu.VMEM((rows, columns), BF16), pltpu.VMEM(part.shape, BF16), dma((8,)), dma((2,))],
        compiler_params=pltpu.CompilerParams(vmem_limit_bytes=VMEM_LIMIT),
        cost_estimate=pl.CostEstimate(flops=rows * depth * columns, bytes_accessed=1 << 26, transcendentals=0),
        name="by_w",
    )(xb, g, part)


def solution(mesh):
    n = mesh.shape["tp"]

    def step(x, w, label):
        me, own, columns = lax.axis_index("tp"), x.shape[0], w.shape[1]
        piece = own // PIECES
        lab = jnp.pad(label.reshape(PIECES, piece), ((0, 0), (0, 128 - piece)))
        xb, z, labs, top, inv, loss = logits_call(n, x, w, lab)
        mine = labs[:, :, :piece].reshape(n // 2, 2, PIECES, piece).swapaxes(1, 2).reshape(-1, 128) - me * columns
        by_x, g, part, *_ = scatter_call(n, z, w, xb.reshape(-1, xb.shape[-1]), top, inv, mine.astype(F32))
        by_w = by_w_call(xb.reshape(-1, xb.shape[-1]), g.reshape(-1, columns), part)
        by_device = loss.reshape(n // 2, PIECES, 2, piece).swapaxes(1, 2).reshape(n, own)
        return lax.dynamic_index_in_dim(by_device, me, 0, keepdims=False), by_x, by_w

    return jax.shard_map(
        step,
        mesh=mesh,
        in_specs=(P(("dp", "tp"), None), P(None, "tp"), P(("dp", "tp"))),
        out_specs=(P(("dp", "tp")), P(("dp", "tp"), None), P("dp", "tp")),
        check_vma=False,
    )
```

time: 575 us -> 479 us (0.83)
  Pallas kernels: 0 us -> 467 us
  matrix products: 306 us -> 0 us
  waiting for transfers between devices: 156 us -> 0 us
  blocking collectives: 49.6 us -> 0 us
  local copies, waits for them, and re-layouts: 33.5 us -> 6.79 us
  other arithmetic: 14.9 us -> 0.76 us
  between operations: 14.1 us -> 0.68 us
    pallas_call x0 -> x3, Pallas kernels: none -> 467 us  [the longest x1 230 us: scatter_call(): pl.pallas_call(functools.partial(scatter_kernel, n), in_specs=[anywhere,...]
    dot_general x3 -> x0, matrix products: 306 us -> none  [the longest x1 126 us: step(): jnp.dot(rows.T, by_logits, preferred_element_type=jnp.float32)]
    all_gather x1 -> x0, waiting for transfers between devices: 114 us -> none  [step(): rows = lax.all_gather(x, 'tp', axis=0, tiled=True)]
    reduce_scatter x1 -> x0, waiting for transfers between devices: 40.9 us -> none  [step(): by_x = lax.psum_scatter(term, 'tp', scatter_dimension=0, tiled=True)]
    unnamed x1 -> x0, blocking collectives: 35.4 us -> none
    unnamed x5 -> x1, local copies, waits for them, and re-layouts: 33.5 us -> 3.3 us
    all_gather x1 -> x0, blocking collectives: 14.2 us -> none  [step(): high, sums, right = jnp.moveaxis(lax.all_gather(own, 'tp'), 1, 0)]
    reduce_sum x2 -> x0, other arithmetic: 11.8 us -> none  [the longest x1 11.7 us: step(): jnp.sum(jnp.exp(logits - high[:, None]), -1)]
  transfers between devices with their start and end apart: 2 -> 0, of which waited for: 2 -> 0; matrix products, arithmetic and copies ran while one was open for 28% -> 0% of each run, Pallas kernels for 0% -> 0%
where the time goes in v2:
time: 479 us; the launch traced here: 475 us
  Pallas kernels  467 us (97%)
  local copies, waits for them, and re-layouts  6.79 us (1%)
    pallas_call x1, Pallas kernels, scatter_call(): pl.pallas_call(functools.partial(scatter_kernel, n), in_specs=[anywhere,...  230 us
    pallas_call x1, Pallas kernels, logits_call(): pl.pallas_call(functools.partial(logits_kernel, n), in_specs=[anywhere, a...  175 us
    pallas_call x1, Pallas kernels, by_w_call(): pl.pallas_call(by_w_kernel, in_specs=[anywhere] * 3, out_specs=anywhere,...  61.4 us

profile of v2, /device:TPU:0, one launch (start us, length us, event | category | flops | bytes accessed | tf_op | source)
XLA Modules:
  0.0 475.1 jit_solution(3920611333092290083)
XLA Ops:
  0.6 0.8 reshape.30
  1.4 0.6 pad.4.lab_ref
  2.0 175.1 %gather_logits.1 = (bf16[8,384,6144]{2,1,0:T(8,128)(2,1)}, f32[8,384,2048]{2,1,0:T(8,128)}, s32[16,3,128]{2,1,0:T(4,128)}, f32[24,128]{1,0:T(8,128)}, f32[24,128]{1,0:T(8,128)}, /*index=5*/f32[24,128]{1,0:T(8,128)}) custom-call(bf16[192,6144]{1,0:T(8,128)(2,1)} %x_ref.1, bf16[6144,2048]{1,0:T(8,128)(2,1)} %w_ref.3, s32[3,128]{1,0:T(4,128)} %pad.4.lab_ref), custom_call_target="tpu_custom_call" | custom-call | flops 77309411328 | bytes 134217728 | tf_op jit(solution)/shard_map/gather_logits/pallas_call | solution.py:248
  177.1 0.8 reshape.31
  177.9 0.1 reshape.32
  178.0 0.6 constant_dynamic-slice_fusion
  178.6 0.8 subtract_convert_fusion
  179.3 0.7 convert_element_type.12.lab_ref
  180.0 230.3 %by_x_scatter.1 = (bf16[192,6144]{1,0:T(8,128)(2,1)}, bf16[8,384,2048]{2,1,0:T(8,128)(2,1)}, bf16[2560,2048]{1,0:T(8,128)(2,1)}, bf16[8,192,6144]{2,1,0:T(8,128)...) custom-call(f32[8,384,2048]{2,1,0:T(8,128)} %get-tuple-element.13.z_, ...), custom_call_target="tpu_custom_call" | custom-call | flops 115964116992 | bytes 268435456 | tf_op jit(solution)/shard_map/by_x_scatter/pallas_call | solution.py:472
  410.4 61.4 %by_w.1 = bf16[6144,2048]{1,0:T(8,128)(2,1)} custom-call(bf16[3072,6144]{1,0:T(8,128)(2,1)} %bitcast.15, bf16[3072,2048]{1,0:T(8,128)(2,1)} %bitcast.16, bf16[2560,2048]{1,0:T(8,128)(2,1)} %get-tuple-element.20.part_ref), custom_call_target="tpu_custom_call" | custom-call | flops 38654705664 | bytes 67108864 | tf_op jit(solution)/shard_map/by_w/pallas_call | solution.py:548
  471.8 3.3 copy.14
  (2 shorter events, 0.0 us)

commit v3 on v2

--- a/solution.py
+++ b/solution.py
@@ -133,8 +133,6 @@
         kept[-1].start()
     for copy in labels:
         copy.wait_recv()
-    for copy in w_copies:
-        copy.wait()
 
     z_copies = {0: [], 1: []}
     lane = lax.broadcasted_iota(jnp.int32, (half, 128), 1)
@@ -192,26 +190,43 @@
             copies[-1].start()
         return copies
 
+    def wait(copies):
+        for copy in copies:
+            copy.wait()
+
+    def load_shared(k):
+        for i in range(PIECES):
+            sent["pair", k, i].wait_recv()
+        return load(k, 1)
+
+    def arrive(k):
+        for i in range(PIECES):
+            sent["ici", k, i].wait_recv()
+        for i in range(PIECES):
+            for later in range(4, BATCHES):
+                if BEFORE[later] == k:
+                    send(later, i)
+        for i in range(PIECES):
+            share(k, i)
+        return load(k, 0)
+
+    last = BATCHES - 1
+    own_load, shared_load = [], load_shared(0)
+    wait(w_copies)
     for k in range(BATCHES):
-        if k > 0:
-            for i in range(PIECES):
-                sent["ici", k, i].wait_recv()
-            for i in range(PIECES):
-                for later in range(4, BATCHES):
-                    if BEFORE[later] == k:
-                        send(later, i)
-                share(k, i)
-            for copy in load(k, 0):
-                copy.wait()
         compute(k, 0)
-        for i in range(PIECES):
-            sent["pair", k, i].wait_recv()
         if k == 0:
-            for copy in kept:
-                copy.wait()
-        for copy in load(k, 1):
-            copy.wait()
+            wait(kept)
+        if k + 1 < last:
+            own_load = arrive(k + 1)
+        if k == last:
+            shared_load = load_shared(k)
+        wait(shared_load)
         compute(k, 1)
+        if k + 1 == last:
+            own_load = arrive(last)
+        elif k < last:
+            shared_load = load_shared(k + 1)
         for i in range(PIECES):
             part = pl.ds(i * piece, piece)
             first, second = st_s[0, part, :], st_s[1, part, :]
@@ -221,6 +236,8 @@
             pair = lax.div(flip(me, 2 * MASKS[i][k]), 2) * PIECES + i
             for t in range(3):
                 own_s[t, pl.ds(pair, 1), :] = both[t : t + 1, :]
+        if k < last:
+            wait(own_load)
 
     stats = to_all(n, me, own_s, all_s, st_send, st_recv)
     all_s[me] = own_s[...]
@@ -287,7 +304,7 @@
     )(x, w, lab)
 
 
-PASSES = (((7,), ()), ((6, 5), (7,)), ((4, 3), (6, 5)), ((2, 1), (4, 3)), ((0,), (2, 1)), ((), (0,)))
+PASSES = tuple((7 - t if t < 8 else None, 8 - t if t > 0 else None) for t in range(9))
 
 
 def joins(k):
@@ -296,20 +313,31 @@
 
 def scatter_kernel(
     n, z_ref, w_ref, x_ref, top_ref, inv_ref, lab_ref,
-    out_ref, g_ref, part_ref, give_ref, took_ref, pass_ref, came_ref, last_ref,
-    z_v, g_v, top_s, inv_s, off_s, gw_v, z_sem, g_sem, gw_sem, pair_send, pair_recv, ici_send, ici_recv,
+    out_ref, g_ref, part_ref, took_ref, pass_ref, came_ref,
+    z_v, g_v, w_v, in_v, p_v, o_v, last_v, fin_v, top_s, inv_s, off_s, gw_v,
+    z_sem, g_sem, w_sem, in_sem, p_sem, o_sem, fin_sem, gw_sem, pair_recv, ici_send, ici_recv,
 ):
     me = lax.axis_index("tp")
     core = lax.rem(me, 2)
     half = z_ref.shape[1] // 2
     piece = half // PIECES
     depth, columns = w_ref.shape
-    wide = 512
-
-    groups = [[(k, 1) for k in given] + [(k, 0) for k in own] for given, own in PASSES]
+    wide = w_v.shape[1]
+    steps = depth // wide
+
+    groups = [[(k, other) for k, other in ((given, 1), (own, 0)) if k is not None] for given, own in PASSES]
     flat = [group for one in groups for group in one]
 
-    def load(number):
+    def start(copies):
+        for copy in copies:
+            copy.start()
+        return copies
+
+    def wait(copies):
+        for copy in copies:
+            copy.wait()
+
+    def load_z(number):
         k, other = flat[number]
         return [
             pltpu.make_async_copy(
@@ -320,32 +348,34 @@
             for i in range(PIECES)
         ]
 
-    def start(copies):
-        for copy in copies:
-            copy.start()
-        return copies
-
-    loading = start(load(0))
+    def columns_at(j):
+        return pl.ds(pl.multiple_of(j * wide, wide), wide)
+
+    def load_w(j, slot):
+        return pltpu.make_async_copy(w_ref.at[columns_at(j)], w_v.at[slot], w_sem.at[slot])
+
+    loading = start(load_z(0))
+    load_w(0, 0).start()
     meet(n, me)
 
     lane = lax.broadcasted_iota(jnp.int32, (32, 128), 1)
-    sent = {}
+    sent, load_g = {}, []
     number = 0
-    for given, own in PASSES:
-        rows = half * (len(given) + len(own))
+    for t, (given, own) in enumerate(PASSES):
+        places = {group: place for place, group in enumerate(groups[t])}
+        rows = half * len(places)
         g_copies = []
-        for place, (k, other) in enumerate([(k, 1) for k in given] + [(k, 0) for k in own]):
+        for (k, other), place in places.items():
             for i in range(PIECES):
                 pair = lax.div(flip(me, 2 * MASKS[i][k]), 2) * PIECES + i
                 for from_ref, to_ref in ((top_ref, top_s), (inv_ref, inv_s), (lab_ref, off_s)):
                     both = as_column(from_ref[pl.ds(pair, 1), :])
                     to_ref[pl.ds(i * piece, piece), :] = jnp.where(core == other, both[:piece], both[piece:])
-            for copy in loading:
-                copy.wait()
+            wait(loading)
             slot = number % 2
             number += 1
             if number < len(flat):
-                loading = start(load(number))
+                loading = start(load_z(number))
 
             def body(b, carry, slot=slot, place=place):
                 part = pl.ds(pl.multiple_of(b * 32, 32), 32)
@@ -368,71 +398,107 @@
                 g_copies[-1].start()
 
         arrivals = []
-        for k in own:
-            sent["pair", k].wait_recv()
-            arrivals.append(took_ref.at[k])
-            if k > 0:
-                for b in joins(k):
-                    for i in range(PIECES):
-                        sent["ici", b, i].wait_recv()
-                    arrivals.append(came_ref.at[b])
-        results = [give_ref.at[k] for k in given] + [pass_ref.at[k] if k > 0 else last_ref for k in own]
-
-        def multiply(*refs, given=given, own=own, rows=rows):
-            w_tile, refs = refs[0], list(refs[1:])
-            term = dot(g_v[:rows, :], w_tile[...], ((1,), (1,)))
-            place = 0
-            taken = len(own) + sum(len(joins(k)) for k in own if k > 0)
-            ins, outs = refs[:taken], refs[taken:]
-            for _ in given:
-                outs.pop(0)[...] = term[place : place + half].astype(BF16)
-                place += half
-            for k in own:
-                value = term[place : place + half]
-                for _ in range(1 + (len(joins(k)) if k > 0 else 0)):
-                    value = value + ins.pop(0)[...].astype(F32)
-                out = outs.pop(0)
-                out[...] = value.astype(out.dtype)
-                place += half
-
-        tile = pl.BlockSpec((half, wide), lambda j: (0, j))
-        pltpu.emit_pipeline(
-            multiply,
-            grid=(depth // wide,),
-            in_specs=[pl.BlockSpec((wide, columns), lambda j: (j, 0))] + [tile] * len(arrivals),
-            out_specs=[tile] * len(results),
-        )(w_ref, *arrivals, *results)
-        for copy in g_copies:
-            copy.wait()
-        for k in own:
-            if k > 0:
+        if own is not None:
+            pltpu.make_async_remote_copy(
+                src_ref=took_ref.at[own],
+                dst_ref=took_ref.at[own],
+                send_sem=p_sem.at[0],
+                recv_sem=pair_recv.at[own],
+                device_id={"tp": flip(me, 1)},
+                device_id_type=MESH,
+            ).wait_recv()
+            arrivals.append(took_ref.at[own])
+            for b in joins(own) if own else ():
                 for i in range(PIECES):
-                    part = pl.ds(i * piece, piece)
-                    sent["ici", k, i] = pltpu.make_async_remote_copy(
-                        src_ref=pass_ref.at[k, part],
-                        dst_ref=came_ref.at[k, part],
-                        send_sem=ici_send.at[k, i],
-                        recv_sem=ici_recv.at[k, i],
-                        device_id=across(me, i, k),
+                    sent[b, i].wait_recv()
+                arrivals.append(came_ref.at[b])
+
+        def load_in(j, slot, arrivals=arrivals):
+            return [
+                pltpu.make_async_copy(ref.at[:, columns_at(j)], in_v.at[slot, m], in_sem.at[slot, m])
+                for m, ref in enumerate(arrivals)
+            ]
+
+        def outs(j, slot, given=given, own=own):
+            copies = []
+            if given is not None:
+                copies.append(
+                    pltpu.make_async_remote_copy(
+                        src_ref=p_v.at[slot],
+                        dst_ref=took_ref.at[given, :, columns_at(j)],
+                        send_sem=p_sem.at[slot],
+                        recv_sem=pair_recv.at[given],
+                        device_id={"tp": flip(me, 1)},
                         device_id_type=MESH,
                     )
-                    sent["ici", k, i].start()
-        for k in given:
-            sent["pair", k] = pltpu.make_async_remote_copy(
-                src_ref=give_ref.at[k],
-                dst_ref=took_ref.at[k],
-                send_sem=pair_send.at[k],
-                recv_sem=pair_recv.at[k],
-                device_id={"tp": flip(me, 1)},
-                device_id_type=MESH,
-            )
-            sent["pair", k].start()
-
-    load_g = [
-        pltpu.make_async_copy(g_ref.at[k], gw_v.at[pl.ds(k * 2 * half, 2 * half)], gw_sem.at[k]) for k in range(BATCHES)
-    ]
-    for copy in start(load_g):
-        copy.wait()
+                )
+            if own:
+                copies.append(pltpu.make_async_copy(o_v.at[slot], pass_ref.at[own, :, columns_at(j)], o_sem.at[slot]))
+            return copies
+
+        def finished(copies, given=given):
+            for m, copy in enumerate(copies):
+                if m == 0 and given is not None:
+                    copy.wait_send()
+                else:
+                    copy.wait()
+
+        start(load_in(0, 0))
+
+        def multiply(j, carry, t=t, given=given, own=own, rows=rows, load_in=load_in, outs=outs, finished=finished, count=len(arrivals)):
+            slot = lax.rem(j, 2)
+            if t < len(PASSES) - 1:
+                load_w(lax.rem(j + 1, steps), 1 - slot).start()
+
+            @pl.when(j + 1 < steps)
+            def _():
+                if t == len(PASSES) - 1:
+                    load_w(j + 1, 1 - slot).start()
+                start(load_in(j + 1, 1 - slot))
+
+            @pl.when(j > 0)
+            def _():
+                start(outs(j - 1, 1 - slot))
+
+            @pl.when(j > 1)
+            def _():
+                finished(outs(j - 2, slot))
+
+            load_w(j, slot).wait()
+            wait(load_in(j, slot))
+            term = dot(g_v[:rows, :], w_v[slot], ((1,), (1,)))
+            if given is not None:
+                p_v[slot] = term[:half].astype(BF16)
+            if own is not None:
+                value = term[rows - half :]
+                for m in range(count):
+                    value = value + in_v[slot, m].astype(F32)
+                if own:
+                    o_v[slot] = value.astype(BF16)
+                else:
+                    last_v[:, columns_at(j)] = value
+            return carry
+
+        lax.fori_loop(0, steps, multiply, 0)
+        start(outs(steps - 1, (steps - 1) % 2))
+        for j in (steps - 2, steps - 1):
+            finished(outs(j, j % 2))
+        wait(g_copies)
+        if own is not None:
+            for i in range(PIECES if own else 0):
+                part = pl.ds(i * piece, piece)
+                sent[own, i] = pltpu.make_async_remote_copy(
+                    src_ref=pass_ref.at[own, part],
+                    dst_ref=came_ref.at[own, part],
+                    send_sem=ici_send.at[own, i],
+                    recv_sem=ici_recv.at[own, i],
+                    device_id=across(me, i, own),
+                    device_id_type=MESH,
+                )
+                sent[own, i].start()
+            load_g += start([pltpu.make_async_copy(g_ref.at[own], gw_v.at[pl.ds(own * 2 * half, 2 * half)], gw_sem.at[own])])
+
+    wait(load_g)
 
     def outer(x_tile, out_tile):
         out_tile[...] = dot(x_tile[...], gw_v[...], ((0,), (0,))).astype(BF16)
@@ -444,35 +510,38 @@
         out_specs=[pl.BlockSpec((BY_W_TALL, columns), lambda j: (j, 0))],
     )(x_ref, part_ref)
 
-    for b in joins(0):
-        for i in range(PIECES):
-            sent["ici", b, i].wait_recv()
-
-    def finish(last, *refs):
-        value = last[...]
-        for ref in refs[:-1]:
-            value = value + ref[...].astype(F32)
-        refs[-1][...] = value.astype(BF16)
-
-    tile = pl.BlockSpec((half, 1024), lambda j: (0, j))
-    pltpu.emit_pipeline(
-        finish, grid=(depth // 1024,), in_specs=[tile] * (1 + len(joins(0))), out_specs=[tile]
-    )(last_ref, *[came_ref.at[b] for b in joins(0)], out_ref)
+    ends = []
+    for m, b in enumerate(reversed(joins(0))):
+        for i in range(PIECES):
+            sent[b, i].wait_recv()
+        ends += start([pltpu.make_async_copy(came_ref.at[b], fin_v.at[m], fin_sem.at[m])])
+    wait(ends)
+
+    def finish(j, carry):
+        at = columns_at(j)
+        value = last_v[:, at]
+        for m in range(len(joins(0))):
+            value = value + fin_v[m, :, at].astype(F32)
+        fin_v[0, :, at] = value.astype(BF16)
+        return carry
+
+    lax.fori_loop(0, steps, finish, 0)
+    wait(start([pltpu.make_async_copy(fin_v.at[0], out_ref, fin_sem.at[0])]))
     for copy in sent.values():
         copy.wait_send()
 
 
 def scatter_call(n, z, w, xb, top, inv, lab):
     depth, columns = w.shape
-    half = z.shape[1] // 2
+    half, wide = z.shape[1] // 2, 512
     anywhere, vmem = pl.BlockSpec(memory_space=pl.ANY), pl.BlockSpec(memory_space=pltpu.VMEM)
     dma = pltpu.SemaphoreType.DMA
     moved = jax.ShapeDtypeStruct((BATCHES, half, depth), BF16)
-    most = max(len(given) + len(own) for given, own in PASSES)
+    most = 1 + max(len(joins(k)) for k in range(1, BATCHES))
     return pl.pallas_call(
         functools.partial(scatter_kernel, n),
         in_specs=[anywhere, anywhere, anywhere, vmem, vmem, vmem],
-        out_specs=[anywhere] * 8,
+        out_specs=[anywhere] * 6,
         out_shape=[
             jax.ShapeDtypeStruct((half, depth), BF16),
             jax.ShapeDtypeStruct(z.shape, BF16),
@@ -480,19 +549,27 @@
             moved,
             moved,
             moved,
-            moved,
-            jax.ShapeDtypeStruct((half, depth), F32),
         ],
         scratch_shapes=[
             pltpu.VMEM((2, half, columns), F32),
-            pltpu.VMEM((most * half, columns), BF16),
+            pltpu.VMEM((2 * half, columns), BF16),
+            pltpu.VMEM((2, wide, columns), BF16),
+            pltpu.VMEM((2, most, half, wide), BF16),
+            pltpu.VMEM((2, half, wide), BF16),
+            pltpu.VMEM((2, half, wide), BF16),
+            pltpu.VMEM((half, depth), F32),
+            pltpu.VMEM((len(joins(0)), half, depth), BF16),
             pltpu.VMEM((half, 128), F32),
             pltpu.VMEM((half, 128), F32),
             pltpu.VMEM((half, 128), F32),
             pltpu.VMEM((BATCHES * 2 * half, columns), BF16),
             dma((2, PIECES)),
-            dma((most, PIECES)),
-            dma((BATCHES,)),
+            dma((2, PIECES)),
+            dma((2,)),
+            dma((2, most)),
+            dma((2,)),
+            dma((2,)),
+            dma((3,)),
             dma((BATCHES,)),
             dma((BATCHES,)),
             dma((BATCHES, PIECES)),

time: 479 us -> 477 us (level)
  no operation moved by 1% of the time
where the time goes in v3:
time: 477 us; the launch traced here: 475 us
  Pallas kernels  466 us (98%)
  local copies, waits for them, and re-layouts  6.79 us (1%)
    pallas_call x1, Pallas kernels, scatter_call(): pl.pallas_call(functools.partial(scatter_kernel, n), in_specs=[anywhere,...  234 us
    pallas_call x1, Pallas kernels, logits_call(): pl.pallas_call(functools.partial(logits_kernel, n), in_specs=[anywhere, a...  171 us
    pallas_call x1, Pallas kernels, by_w_call(): pl.pallas_call(by_w_kernel, in_specs=[anywhere] * 3, out_specs=anywhere,...  61.4 us

profile of v3, /device:TPU:0, one launch (start us, length us, event | category | flops | bytes accessed | tf_op | source)
XLA Modules:
  0.0 474.6 jit_solution(7917688951358803377)
XLA Ops:
  0.6 0.8 reshape.30
  1.4 0.6 pad.4.lab_ref
  2.0 171.3 %gather_logits.1 = (bf16[8,384,6144]{2,1,0:T(8,128)(2,1)}, f32[8,384,2048]{2,1,0:T(8,128)}, s32[16,3,128]{2,1,0:T(4,128)}, f32[24,128]{1,0:T(8,128)}, f32[24,128]{1,0:T(8,128)}, /*index=5*/f32[24,128]{1,0:T(8,128)}) custom-call(bf16[192,6144]{1,0:T(8,128)(2,1)} %x_ref.1, bf16[6144,2048]{1,0:T(8,128)(2,1)} %w_ref.3, s32[3,128]{1,0:T(4,128)} %pad.4.lab_ref), custom_call_target="tpu_custom_call" | custom-call | flops 77309411328 | bytes 134217728 | tf_op jit(solution)/shard_map/gather_logits/pallas_call | solution.py:265
  173.3 0.8 reshape.31
  174.1 0.1 reshape.32
  174.2 0.6 constant_dynamic-slice_fusion
  174.8 0.8 subtract_convert_fusion
  175.6 0.7 convert_element_type.12.lab_ref
  176.3 233.6 %by_x_scatter.1 = (bf16[192,6144]{1,0:T(8,128)(2,1)}, bf16[8,384,2048]{2,1,0:T(8,128)(2,1)}, bf16[2560,2048]{1,0:T(8,128)(2,1)}, bf16[8,192,6144]{2,1,0:T(8,128)...) custom-call(f32[8,384,2048]{2,1,0:T(8,128)} %get-tuple-element.13.z_ref, bf16[6144,2048]{1,0:T(8,128)(2,1)} %w_ref.3, ...), custom_call_target="tpu_custom_call" | custom-call | flops 115964116992 | bytes 268435456 | tf_op jit(solution)/shard_map/by_x_scatter/pallas_call | solution.py:541
  409.8 61.4 %by_w.1 = bf16[6144,2048]{1,0:T(8,128)(2,1)} custom-call(bf16[3072,6144]{1,0:T(8,128)(2,1)} %bitcast.15, bf16[3072,2048]{1,0:T(8,128)(2,1)} %bitcast.16, bf16[2560,2048]{1,0:T(8,128)(2,1)} %get-tuple-element.20.part_ref), custom_call_target="tpu_custom_call" | custom-call | flops 38654705664 | bytes 67108864 | tf_op jit(solution)/shard_map/by_w/pallas_call | solution.py:625
  471.3 3.3 copy.14
  (2 shorter events, 0.0 us)

commit v4 on v3

--- a/solution.py
+++ b/solution.py
@@ -12,9 +12,8 @@
 VMEM_LIMIT = 63 * 1024 * 1024
 
 ORDERS = ((4, 2, 1), (2, 1, 4), (1, 4, 2))
-MASKS = tuple((0, a, b, c, a | b, a | c, b | c, a | b | c) for a, b, c in ORDERS)
-LAST = (None, 0, 1, 2, 1, 2, 2, 2)
-BEFORE = (None, 0, 0, 0, 1, 1, 2, 4)
+LAST = (None, 0, 1, 1, 2, 2, 2, 2)
+BEFORE = (None, 0, 0, 1, 0, 1, 2, 3)
 BATCHES, PIECES = 8, 3
 BY_W_TALL = 256
 BY_W_EARLY = 10
@@ -31,6 +30,13 @@
     return index
 
 
+def source_of(me, k, i):
+    index = me
+    for bit, on in zip(ORDERS[i], (lax.rem(k, 2), lax.rem(lax.div(k, 2), 2), lax.div(k, 4))):
+        index = index + on * (2 * bit) * (1 - 2 * lax.rem(lax.div(me, 2 * bit), 2))
+    return index
+
+
 def across(me, i, k):
     return {"tp": flip(me, 2 * ORDERS[i][LAST[k]])}
 
@@ -42,19 +48,19 @@
     pl.semaphore_wait(barrier, n - 1)
 
 
+def all_copy(n, me, own_ref, all_ref, send_sems, recv_sems, j):
+    return pltpu.make_async_remote_copy(
+        src_ref=own_ref,
+        dst_ref=all_ref.at[me],
+        send_sem=send_sems.at[j],
+        recv_sem=recv_sems.at[j],
+        device_id={"tp": lax.rem(me + j, n)},
+        device_id_type=MESH,
+    )
+
+
 def to_all(n, me, own_ref, all_ref, send_sems, recv_sems):
-    copies = []
-    for j in range(1, n):
-        copies.append(
-            pltpu.make_async_remote_copy(
-                src_ref=own_ref,
-                dst_ref=all_ref.at[me],
-                send_sem=send_sems.at[j],
-                recv_sem=recv_sems.at[j],
-                device_id={"tp": lax.rem(me + j, n)},
-                device_id_type=MESH,
-            )
-        )
+    copies = [all_copy(n, me, own_ref, all_ref, send_sems, recv_sems, j) for j in range(1, n)]
     for copy in copies:
         copy.start()
     return copies
@@ -65,25 +71,37 @@
 
 
 def logits_kernel(
-    n, x_ref, w_ref, lab_ref, xb_ref, z_ref, labs_ref, top_ref, inv_ref, loss_ref,
-    w_v, x_v, z_v, m_s, s_s, r_s, off_s, st_s, own_s, all_s,
+    n, x_ref, w_ref, lab_ref, xb_ref, z_ref, rel_ref, top_ref, inv_ref, loss_ref,
+    w_v, x_v, z_v, m_s, s_s, r_s, off_s, st_s, own_s, all_s, end_s, ends_s, labs_s,
     w_sem, x_sem, keep_sem, z_sem, ici_send, ici_recv, pair_send, pair_recv, lab_send, lab_recv, st_send, st_recv,
+    end_send, end_recv,
 ):
     me = lax.axis_index("tp")
     core = lax.rem(me, 2)
     piece = x_ref.shape[0] // PIECES
     half = PIECES * piece
     depth, columns = w_ref.shape
-    wide = 256
+    wide = 1024
+    last = BATCHES - 1
+
+    def start(copies):
+        for copy in copies:
+            copy.start()
+        return copies
+
+    def wait(copies):
+        for copy in copies:
+            copy.wait()
 
     w_parts = 8
     w_copies = []
     for p in range(w_parts):
         part = pl.ds(p * (depth // w_parts), depth // w_parts)
         w_copies.append(pltpu.make_async_copy(w_ref.at[part], w_v.at[part], w_sem.at[p]))
-        w_copies[-1].start()
     x_load = pltpu.make_async_copy(x_ref, x_v.at[0], x_sem.at[0, 0])
-    x_load.start()
+    start([x_load] + w_copies)
+    own_s[...] = jnp.zeros(own_s.shape, F32)
+    end_s[...] = jnp.zeros(end_s.shape, F32)
 
     meet(n, me)
 
@@ -93,10 +111,8 @@
     def source(k, i):
         return x_ref.at[pl.ds(i * piece, piece)] if k == 0 else slot(k, i, 0)
 
-    sent = {}
-
     def send(k, i):
-        sent["ici", k, i] = pltpu.make_async_remote_copy(
+        return pltpu.make_async_remote_copy(
             src_ref=source(BEFORE[k], i),
             dst_ref=slot(k, i, 0),
             send_sem=ici_send.at[k, i],
@@ -104,49 +120,68 @@
             device_id=across(me, i, k),
             device_id_type=MESH,
         )
-        sent["ici", k, i].start()
-
-    def share(k, i):
-        sent["pair", k, i] = pltpu.make_async_remote_copy(
-            src_ref=source(k, i),
+
+    def share(k, i, from_x=False):
+        return pltpu.make_async_remote_copy(
+            src_ref=source(0, i) if from_x else slot(k, i, 0),
             dst_ref=slot(k, i, 1),
             send_sem=pair_send.at[k, i],
             recv_sem=pair_recv.at[k, i],
             device_id={"tp": flip(me, 1)},
             device_id_type=MESH,
         )
-        sent["pair", k, i].start()
-
-    labels = to_all(n, me, lab_ref, labs_ref, lab_send, lab_recv)
-    for i in range(PIECES):
-        send(1, i)
-    for i in range(PIECES):
-        share(0, i)
-    for k in (2, 3):
-        for i in range(PIECES):
-            send(k, i)
-    labs_ref[me] = lab_ref[...]
+
+    labels = to_all(n, me, lab_ref, labs_s, lab_send, lab_recv)
+    start([send(1, i) for i in range(PIECES)])
+    start([share(0, i, True) for i in range(PIECES)])
+    for k in (2, 4):
+        start([send(k, i) for i in range(PIECES)])
+    labs_s[me] = lab_ref[...]
     x_load.wait()
-    kept = []
-    for i in range(PIECES):
-        kept.append(pltpu.make_async_copy(x_v.at[0, pl.ds(i * piece, piece)], slot(0, i, 0), keep_sem.at[i]))
-        kept[-1].start()
+    kept = start(
+        [pltpu.make_async_copy(x_v.at[0, pl.ds(i * piece, piece)], slot(0, i, 0), keep_sem.at[i]) for i in range(PIECES)]
+    )
     for copy in labels:
         copy.wait_recv()
-
-    z_copies = {0: [], 1: []}
+    low = lax.broadcasted_iota(jnp.int32, (1, 128), 1) < piece
+    for chip in range(n // 2):
+        for i in range(PIECES):
+            first, second = labs_s[2 * chip, i : i + 1, :].astype(F32), labs_s[2 * chip + 1, i : i + 1, :].astype(F32)
+            rel_ref[chip * PIECES + i : chip * PIECES + i + 1, :] = (
+                jnp.where(low, first, pltpu.roll(second, piece, 1)) - (me * columns).astype(F32)
+            )
+
     lane = lax.broadcasted_iota(jnp.int32, (half, 128), 1)
+
+    def load(k, other):
+        return [
+            pltpu.make_async_copy(slot(k, i, other), x_v.at[other, pl.ds(i * piece, piece)], x_sem.at[other, i])
+            for i in range(PIECES)
+        ]
+
+    def store_z(k, other):
+        return [
+            pltpu.make_async_copy(
+                z_v.at[other, pl.ds(i * piece, piece)],
+                z_ref.at[k, pl.ds(i * 2 * piece + other * piece, piece)],
+                z_sem.at[other, i],
+            )
+            for i in range(PIECES)
+        ]
 
     def compute(k, other):
         for i in range(PIECES):
-            dev = flip(me, 2 * MASKS[i][k] + other)
-            row = (labs_ref[dev, pl.ds(i, 1), :] - me * columns).astype(F32)
+            dev = source_of(me, k, i)
+            dev = flip(dev, 1) if other else dev
+            row = (labs_s[dev, pl.ds(i, 1), :] - me * columns).astype(F32)
             off_s[pl.ds(i * piece, piece), :] = as_column(row)[:piece].astype(jnp.int32)
         m_s[...] = jnp.full(m_s.shape, -jnp.inf, F32)
         s_s[...] = jnp.zeros(s_s.shape, F32)
         r_s[...] = jnp.zeros(r_s.shape, F32)
-        for copy in z_copies[other]:
-            copy.wait()
+
+        @pl.when(k > 0)
+        def _():
+            wait(store_z(k, other))
 
         def body(j, carry):
             at = pl.multiple_of(j * wide, wide)
@@ -168,92 +203,106 @@
             return carry
 
         lax.fori_loop(0, columns // wide, body, 0)
-        z_copies[other] = []
-        for i in range(PIECES):
-            z_copies[other].append(
-                pltpu.make_async_copy(
-                    z_v.at[other, pl.ds(i * piece, piece)],
-                    z_ref.at[k, pl.ds(i * 2 * piece + other * piece, piece)],
-                    z_sem.at[other, i],
-                )
-            )
-            z_copies[other][-1].start()
+        start(store_z(k, other))
         high = jnp.max(m_s[...], -1, keepdims=True)
         total = jnp.sum(s_s[...] * jnp.exp(m_s[...] - high), -1, keepdims=True)
         right = jnp.sum(r_s[...], -1, keepdims=True)
         st_s[other] = jnp.where(lane == 0, high, jnp.where(lane == 1, total, jnp.where(lane == 2, right, 0.0)))
 
-    def load(k, other):
-        copies = []
+    def arrive(k):
         for i in range(PIECES):
-            copies.append(pltpu.make_async_copy(slot(k, i, other), x_v.at[other, pl.ds(i * piece, piece)], x_sem.at[other, i]))
-            copies[-1].start()
-        return copies
-
-    def wait(copies):
-        for copy in copies:
-            copy.wait()
+            send(k, i).wait_recv()
+        start([send(later, i) for i in range(PIECES) for later in range(1, BATCHES) if BEFORE[later] == k])
+        start([share(k, i) for i in range(PIECES)])
+        start(load(k, 0))
 
     def load_shared(k):
         for i in range(PIECES):
-            sent["pair", k, i].wait_recv()
-        return load(k, 1)
-
-    def arrive(k):
-        for i in range(PIECES):
-            sent["ici", k, i].wait_recv()
-        for i in range(PIECES):
-            for later in range(4, BATCHES):
-                if BEFORE[later] == k:
-                    send(later, i)
-        for i in range(PIECES):
-            share(k, i)
-        return load(k, 0)
-
-    last = BATCHES - 1
-    own_load, shared_load = [], load_shared(0)
+            share(k, i).wait_recv()
+        start(load(k, 1))
+
+    load_shared(0)
     wait(w_copies)
-    for k in range(BATCHES):
+
+    def batch(k, carry):
         compute(k, 0)
-        if k == 0:
+
+        @pl.when(k == 0)
+        def _():
             wait(kept)
-        if k + 1 < last:
-            own_load = arrive(k + 1)
-        if k == last:
-            shared_load = load_shared(k)
-        wait(shared_load)
+
+        for now in range(1, last):
+
+            @pl.when(k + 1 == now)
+            def _(now=now):
+                arrive(now)
+
+        @pl.when(k == last)
+        def _():
+            to_all(n, me, own_s, all_s, st_send, st_recv)
+            load_shared(last)
+
+        wait(load(k, 1))
         compute(k, 1)
-        if k + 1 == last:
-            own_load = arrive(last)
-        elif k < last:
-            shared_load = load_shared(k + 1)
+
+        @pl.when(k + 1 == last)
+        def _():
+            arrive(last)
+
+        @pl.when(k + 1 < last)
+        def _():
+            load_shared(k + 1)
+
         for i in range(PIECES):
             part = pl.ds(i * piece, piece)
             first, second = st_s[0, part, :], st_s[1, part, :]
             both = jnp.concatenate(
                 [jnp.where(core == 0, first, second), jnp.where(core == 0, second, first)], 0
             ).T
-            pair = lax.div(flip(me, 2 * MASKS[i][k]), 2) * PIECES + i
-            for t in range(3):
-                own_s[t, pl.ds(pair, 1), :] = both[t : t + 1, :]
-        if k < last:
-            wait(own_load)
-
-    stats = to_all(n, me, own_s, all_s, st_send, st_recv)
+            pair = lax.div(source_of(me, k, i), 2) * PIECES + i
+
+            @pl.when(k < last)
+            def _(i=i, both=both, pair=pair):
+                for t in range(3):
+                    own_s[t, pl.ds(pair, 1), :] = both[t : t + 1, :]
+
+            @pl.when(k == last)
+            def _(i=i, both=both):
+                for t in range(3):
+                    end_s[t, i : i + 1, :] = both[t : t + 1, :]
+
+        @pl.when(k < last)
+        def _():
+            wait(load(k + 1, 0))
+
+        return carry
+
+    lax.fori_loop(0, BATCHES, batch, 0)
+
     all_s[me] = own_s[...]
-    for copy in stats:
+    ends_s[me] = end_s[...]
+    ends = to_all(n, me, end_s, ends_s, end_send, end_recv)
+    stats = [all_copy(n, me, own_s, all_s, st_send, st_recv, j) for j in range(1, n)]
+    for copy in stats + ends:
         copy.wait_recv()
+    for dev in range(n):
+        row = (n // 2 - 1 - dev // 2) * PIECES
+        for t in range(3):
+            all_s[dev, t, row : row + PIECES, :] = ends_s[dev, t, :PIECES, :]
     high, sums, right = all_s[:, 0], all_s[:, 1], all_s[:, 2]
     top = jnp.max(high, 0)
     total = jnp.sum(sums * jnp.exp(high - top[None]), 0)
     top_ref[...] = top
     inv_ref[...] = 1.0 / total
     loss_ref[...] = jnp.log(total) + top - jnp.sum(right, 0)
-    for copy in labels + stats + list(sent.values()):
+    for copy in labels + stats + ends:
         copy.wait_send()
-    for copies in z_copies.values():
-        for copy in copies:
-            copy.wait()
+    for k in range(BATCHES):
+        for i in range(PIECES):
+            share(k, i, k == 0).wait_send()
+            if k > 0:
+                send(k, i).wait_send()
+    wait(store_z(last, 0) + store_z(last, 1))
 
 
 def logits_call(n, x, w, lab):
@@ -269,7 +318,7 @@
         out_shape=[
             jax.ShapeDtypeStruct((BATCHES, 2 * own, depth), BF16),
             jax.ShapeDtypeStruct((BATCHES, 2 * own, columns), F32),
-            jax.ShapeDtypeStruct((n,) + lab.shape, jnp.int32),
+            jax.ShapeDtypeStruct((pairs, 128), F32),
             jax.ShapeDtypeStruct((pairs, 128), F32),
             jax.ShapeDtypeStruct((pairs, 128), F32),
             jax.ShapeDtypeStruct((pairs, 128), F32),
@@ -285,6 +334,9 @@
             pltpu.VMEM((2, own, 128), F32),
             pltpu.VMEM((3, pairs, 128), F32),
             pltpu.VMEM((n, 3, pairs, 128), F32),
+            pltpu.VMEM((3, 8, 128), F32),
+            pltpu.VMEM((n, 3, 8, 128), F32),
+            pltpu.VMEM((n,) + lab.shape, jnp.int32),
             dma((8,)),
             dma((2, PIECES)),
             dma((PIECES,)),
@@ -293,6 +345,8 @@
             dma((BATCHES, PIECES)),
             dma((BATCHES, PIECES)),
             dma((BATCHES, PIECES)),
+            dma((n,)),
+            dma((n,)),
             dma((n,)),
             dma((n,)),
             dma((n,)),
@@ -367,7 +421,7 @@
         g_copies = []
         for (k, other), place in places.items():
             for i in range(PIECES):
-                pair = lax.div(flip(me, 2 * MASKS[i][k]), 2) * PIECES + i
+                pair = lax.div(source_of(me, jnp.int32(k), i), 2) * PIECES + i
                 for from_ref, to_ref in ((top_ref, top_s), (inv_ref, inv_s), (lab_ref, off_s)):
                     both = as_column(from_ref[pl.ds(pair, 1), :])
                     to_ref[pl.ds(i * piece, piece), :] = jnp.where(core == other, both[:piece], both[piece:])
@@ -533,7 +587,7 @@
 
 def scatter_call(n, z, w, xb, top, inv, lab):
     depth, columns = w.shape
-    half, wide = z.shape[1] // 2, 512
+    half, wide = z.shape[1] // 2, 1024
     anywhere, vmem = pl.BlockSpec(memory_space=pl.ANY), pl.BlockSpec(memory_space=pltpu.VMEM)
     dma = pltpu.SemaphoreType.DMA
     moved = jax.ShapeDtypeStruct((BATCHES, half, depth), BF16)
@@ -581,7 +635,7 @@
     )(z, w, xb, top, inv, lab)
 
 
-def by_w_kernel(x_ref, g_ref, part_ref, out_ref, g_v, part_v, g_sem, part_sem):
+def by_w_kernel(x_ref, g_ref, part_ref, by_x_ref, out_ref, by_x_out_ref, g_v, part_v, by_x_v, g_sem, part_sem):
     rows, columns = g_ref.shape
     early = part_ref.shape[0]
     g_load = [
@@ -592,6 +646,8 @@
     for copy in g_load:
         copy.start()
     load.start()
+    by_x_load = pltpu.make_async_copy(by_x_ref, by_x_v, part_sem.at[2])
+    by_x_load.start()
     for copy in g_load:
         copy.wait()
 
@@ -613,25 +669,35 @@
     load.wait()
     store = pltpu.make_async_copy(part_v, out_ref.at[pl.ds(0, early)], part_sem.at[1])
     store.start()
+    by_x_load.wait()
+    by_x_store = pltpu.make_async_copy(by_x_v, by_x_out_ref, part_sem.at[3])
+    by_x_store.start()
     run(tiles // 2, tiles - tiles // 2)
     store.wait()
-
-
-def by_w_call(xb, g, part):
+    by_x_store.wait()
+
+
+def by_w_call(xb, g, part, by_x):
     rows, depth = xb.shape
     columns = g.shape[1]
     anywhere = pl.BlockSpec(memory_space=pl.ANY)
     dma = pltpu.SemaphoreType.DMA
     return pl.pallas_call(
         by_w_kernel,
-        in_specs=[anywhere] * 3,
-        out_specs=anywhere,
-        out_shape=jax.ShapeDtypeStruct((depth, columns), BF16),
-        scratch_shapes=[pltpu.VMEM((rows, columns), BF16), pltpu.VMEM(part.shape, BF16), dma((8,)), dma((2,))],
+        in_specs=[anywhere] * 4,
+        out_specs=[anywhere] * 2,
+        out_shape=[jax.ShapeDtypeStruct((depth, columns), BF16), jax.ShapeDtypeStruct(by_x.shape, BF16)],
+        scratch_shapes=[
+            pltpu.VMEM((rows, columns), BF16),
+            pltpu.VMEM(part.shape, BF16),
+            pltpu.VMEM(by_x.shape, BF16),
+            dma((8,)),
+            dma((4,)),
+        ],
         compiler_params=pltpu.CompilerParams(vmem_limit_bytes=VMEM_LIMIT),
         cost_estimate=pl.CostEstimate(flops=rows * depth * columns, bytes_accessed=1 << 26, transcendentals=0),
         name="by_w",
-    )(xb, g, part)
+    )(xb, g, part, by_x)
 
 
 def solution(mesh):
@@ -641,10 +707,9 @@
         me, own, columns = lax.axis_index("tp"), x.shape[0], w.shape[1]
         piece = own // PIECES
         lab = jnp.pad(label.reshape(PIECES, piece), ((0, 0), (0, 128 - piece)))
-        xb, z, labs, top, inv, loss = logits_call(n, x, w, lab)
-        mine = labs[:, :, :piece].reshape(n // 2, 2, PIECES, piece).swapaxes(1, 2).reshape(-1, 128) - me * columns
-        by_x, g, part, *_ = scatter_call(n, z, w, xb.reshape(-1, xb.shape[-1]), top, inv, mine.astype(F32))
-        by_w = by_w_call(xb.reshape(-1, xb.shape[-1]), g.reshape(-1, columns), part)
+        xb, z, rel, top, inv, loss = logits_call(n, x, w, lab)
+        by_x, g, part, *_ = scatter_call(n, z, w, xb.reshape(-1, xb.shape[-1]), top, inv, rel)
+        by_w, by_x = by_w_call(xb.reshape(-1, xb.shape[-1]), g.reshape(-1, columns), part, by_x)
         by_device = loss.reshape(n // 2, PIECES, 2, piece).swapaxes(1, 2).reshape(n, own)
         return lax.dynamic_index_in_dim(by_device, me, 0, keepdims=False), by_x, by_w
 

time: 477 us -> 437 us (0.916)
  Pallas kernels: 466 us -> 432 us
    pallas_call x1, Pallas kernels: 234 us -> 200 us  [scatter_call(): pl.pallas_call(functools.partial(scatter_kernel, n), in_specs=[anywhere,...]
where the time goes in v4:
time: 437 us; the launch traced here: 436 us
  Pallas kernels  432 us (99%)
    pallas_call x1, Pallas kernels, scatter_call(): pl.pallas_call(functools.partial(scatter_kernel, n), in_specs=[anywhere,...  200 us
    pallas_call x1, Pallas kernels, logits_call(): pl.pallas_call(functools.partial(logits_kernel, n), in_specs=[anywhere, a...  170 us
    pallas_call x1, Pallas kernels, by_w_call(): pl.pallas_call(by_w_kernel, in_specs=[anywhere] * 4, out_specs=[anywhere]...  62.4 us

profile of v4, /device:TPU:0, one launch (start us, length us, event | category | flops | bytes accessed | tf_op | source)
XLA Modules:
  0.0 435.9 jit_solution(11039254304905317045)
XLA Ops:
  0.6 0.8 reshape.22
  1.4 0.6 pad.4.lab_ref
  2.0 169.7 %gather_logits.1 = (bf16[8,384,6144]{2,1,0:T(8,128)(2,1)}, f32[8,384,2048]{2,1,0:T(8,128)}, f32[24,128]{1,0:T(8,128)}, f32[24,128]{1,0:T(8,128)}, f32[24,128]{1,0:T(8,128)}, /*index=5*/f32[24,128]{1,0:T(8,128)}) custom-call(bf16[192,6144]{1,0:T(8,128)(2,1)} %x_ref.1, bf16[6144,2048]{1,0:T(8,128)(2,1)} %w_ref.3, s32[3,128]{1,0:T(4,128)} %pad.4.lab_ref), custom_call_target="tpu_custom_call" | custom-call | flops 77309411328 | bytes 134217728 | tf_op jit(solution)/shard_map/gather_logits/pallas_call | solution.py:314
  171.7 0.8 reshape.23
  172.5 0.1 reshape.24
  172.6 0.6 constant_dynamic-slice_fusion
  173.1 200.2 %by_x_scatter.1 = (bf16[192,6144]{1,0:T(8,128)(2,1)}, bf16[8,384,2048]{2,1,0:T(8,128)(2,1)}, bf16[2560,2048]{1,0:T(8,128)(2,1)}, bf16[8,192,6144]{2,1,0:T(8,128)...) custom-call(f32[8,384,2048]{2,1,0:T(8,128)} %get-tuple-element.16.z_ref, bf16[6144,2048]{1,0:T(8,128)(2,1)} %w_ref.3, ...), custom_call_target="tpu_custom_call" | custom-call | flops 115964116992 | bytes 268435456 | tf_op jit(solution)/shard_map/by_x_scatter/pallas_call | solution.py:595
  373.3 62.4 %by_w.1 = (bf16[6144,2048]{1,0:T(8,128)(2,1)}, bf16[192,6144]{1,0:T(8,128)(2,1)}) custom-call(bf16[3072,6144]{1,0:T(8,128)(2,1)} %bitcast.9, bf16[3072,2048]{1,0:T(8,128)(2,1)} %bitcast.10, bf16[2560,2048]{1,0:T(8,128)(2,1)} %get-tuple-element.21.part_ref, bf16[192,6144]{1,0:T(8,128)(2,1)} %get-tuple-element.22.by_x_ref), custom_call_target="tpu_custom_call" | custom-call | flops 38654705664 | bytes 67108864 | tf_op jit(solution)/shard_map/by_w/pallas_call | solution.py:685
  (1 shorter events, 0.0 us)

commit v5 on v4

--- a/solution.py
+++ b/solution.py
@@ -134,8 +134,7 @@
     labels = to_all(n, me, lab_ref, labs_s, lab_send, lab_recv)
     start([send(1, i) for i in range(PIECES)])
     start([share(0, i, True) for i in range(PIECES)])
-    for k in (2, 4):
-        start([send(k, i) for i in range(PIECES)])
+    start([send(2, i) for i in range(PIECES)])
     labs_s[me] = lab_ref[...]
     x_load.wait()
     kept = start(
@@ -212,7 +211,9 @@
     def arrive(k):
         for i in range(PIECES):
             send(k, i).wait_recv()
-        start([send(later, i) for i in range(PIECES) for later in range(1, BATCHES) if BEFORE[later] == k])
+        for later in range(1, BATCHES):
+            if BEFORE[later] == k or (k == 1 and later == 4):
+                start([send(later, i) for i in range(PIECES)])
         start([share(k, i) for i in range(PIECES)])
         start(load(k, 0))
 
@@ -379,9 +380,6 @@
     wide = w_v.shape[1]
     steps = depth // wide
 
-    groups = [[(k, other) for k, other in ((given, 1), (own, 0)) if k is not None] for given, own in PASSES]
-    flat = [group for one in groups for group in one]
-
     def start(copies):
         for copy in copies:
             copy.start()
@@ -391,13 +389,12 @@
         for copy in copies:
             copy.wait()
 
-    def load_z(number):
-        k, other = flat[number]
+    def load_z(k, other, slot):
         return [
             pltpu.make_async_copy(
                 z_ref.at[k, pl.ds(i * 2 * piece + other * piece, piece)],
-                z_v.at[number % 2, pl.ds(i * piece, piece)],
-                z_sem.at[number % 2, i],
+                z_v.at[slot, pl.ds(i * piece, piece)],
+                z_sem.at[slot, i],
             )
             for i in range(PIECES)
         ]
@@ -408,28 +405,44 @@
     def load_w(j, slot):
         return pltpu.make_async_copy(w_ref.at[columns_at(j)], w_v.at[slot], w_sem.at[slot])
 
-    loading = start(load_z(0))
+    def pass_on(k, i, like):
+        part = pl.ds(i * piece, piece)
+        return pltpu.make_async_remote_copy(
+            src_ref=pass_ref.at[k, part],
+            dst_ref=came_ref.at[k, part],
+            send_sem=ici_send.at[k, i],
+            recv_sem=ici_recv.at[k, i],
+            device_id=across(me, i, like),
+            device_id_type=MESH,
+        )
+
+    def load_g(k):
+        to = pl.ds(pl.multiple_of(k * 2 * half, 2 * half), 2 * half)
+        return [pltpu.make_async_copy(g_ref.at[k], gw_v.at[to], gw_sem.at[k])]
+
+    start(load_z(7, 1, 0))
     load_w(0, 0).start()
     meet(n, me)
 
     lane = lax.broadcasted_iota(jnp.int32, (32, 128), 1)
-    sent, load_g = {}, []
-    number = 0
-    for t, (given, own) in enumerate(PASSES):
-        places = {group: place for place, group in enumerate(groups[t])}
-        rows = half * len(places)
+
+    def run_pass(t, given, own, joined, like, after):
+        final = t == len(PASSES) - 1 if isinstance(t, int) else False
+        which = [(given, 1)] if own is None else [(own, 0)] if given is None else [(given, 1), (own, 0)]
+        rows = half * len(which)
         g_copies = []
-        for (k, other), place in places.items():
+        for place, (k, other) in enumerate(which):
+            slot = 0 if own is None else 1 - place
             for i in range(PIECES):
                 pair = lax.div(source_of(me, jnp.int32(k), i), 2) * PIECES + i
                 for from_ref, to_ref in ((top_ref, top_s), (inv_ref, inv_s), (lab_ref, off_s)):
                     both = as_column(from_ref[pl.ds(pair, 1), :])
                     to_ref[pl.ds(i * piece, piece), :] = jnp.where(core == other, both[:piece], both[piece:])
-            wait(loading)
-            slot = number % 2
-            number += 1
-            if number < len(flat):
-                loading = start(load_z(number))
+            wait(load_z(k, other, slot))
+            if place + 1 < len(which):
+                start(load_z(*which[1], 0))
+            elif after is not None:
+                start(load_z(*after, 1))
 
             def body(b, carry, slot=slot, place=place):
                 part = pl.ds(pl.multiple_of(b * 32, 32), 32)
@@ -449,7 +462,7 @@
                         g_sem.at[place, i],
                     )
                 )
-                g_copies[-1].start()
+        start(g_copies)
 
         arrivals = []
         if own is not None:
@@ -462,18 +475,18 @@
                 device_id_type=MESH,
             ).wait_recv()
             arrivals.append(took_ref.at[own])
-            for b in joins(own) if own else ():
+            for b in joined:
                 for i in range(PIECES):
-                    sent[b, i].wait_recv()
+                    pass_on(b, i, b).wait_recv()
                 arrivals.append(came_ref.at[b])
 
-        def load_in(j, slot, arrivals=arrivals):
+        def load_in(j, slot):
             return [
                 pltpu.make_async_copy(ref.at[:, columns_at(j)], in_v.at[slot, m], in_sem.at[slot, m])
                 for m, ref in enumerate(arrivals)
             ]
 
-        def outs(j, slot, given=given, own=own):
+        def outs(j, slot):
             copies = []
             if given is not None:
                 copies.append(
@@ -486,27 +499,30 @@
                         device_id_type=MESH,
                     )
                 )
-            if own:
+            if own is not None and not final:
                 copies.append(pltpu.make_async_copy(o_v.at[slot], pass_ref.at[own, :, columns_at(j)], o_sem.at[slot]))
             return copies
 
-        def finished(copies, given=given):
+        def finished(copies):
             for m, copy in enumerate(copies):
                 if m == 0 and given is not None:
                     copy.wait_send()
                 else:
                     copy.wait()
 
-        start(load_in(0, 0))
-
-        def multiply(j, carry, t=t, given=given, own=own, rows=rows, load_in=load_in, outs=outs, finished=finished, count=len(arrivals)):
-            slot = lax.rem(j, 2)
-            if t < len(PASSES) - 1:
+        def slot_at(j):
+            return lax.rem(jnp.int32(t) * steps + j, 2)
+
+        start(load_in(0, slot_at(0)))
+
+        def multiply(j, carry):
+            slot = slot_at(j)
+            if not final:
                 load_w(lax.rem(j + 1, steps), 1 - slot).start()
 
             @pl.when(j + 1 < steps)
             def _():
-                if t == len(PASSES) - 1:
+                if final:
                     load_w(j + 1, 1 - slot).start()
                 start(load_in(j + 1, 1 - slot))
 
@@ -525,34 +541,43 @@
                 p_v[slot] = term[:half].astype(BF16)
             if own is not None:
                 value = term[rows - half :]
-                for m in range(count):
+                for m in range(len(arrivals)):
                     value = value + in_v[slot, m].astype(F32)
-                if own:
+                if final:
+                    last_v[:, columns_at(j)] = value
+                else:
                     o_v[slot] = value.astype(BF16)
-                else:
-                    last_v[:, columns_at(j)] = value
             return carry
 
         lax.fori_loop(0, steps, multiply, 0)
-        start(outs(steps - 1, (steps - 1) % 2))
+        start(outs(steps - 1, slot_at(steps - 1)))
         for j in (steps - 2, steps - 1):
-            finished(outs(j, j % 2))
+            finished(outs(j, slot_at(j)))
         wait(g_copies)
         if own is not None:
-            for i in range(PIECES if own else 0):
-                part = pl.ds(i * piece, piece)
-                sent[own, i] = pltpu.make_async_remote_copy(
-                    src_ref=pass_ref.at[own, part],
-                    dst_ref=came_ref.at[own, part],
-                    send_sem=ici_send.at[own, i],
-                    recv_sem=ici_recv.at[own, i],
-                    device_id=across(me, i, own),
-                    device_id_type=MESH,
-                )
-                sent[own, i].start()
-            load_g += start([pltpu.make_async_copy(g_ref.at[own], gw_v.at[pl.ds(own * 2 * half, 2 * half)], gw_sem.at[own])])
-
-    wait(load_g)
+            if not final:
+                start([pass_on(own, i, like) for i in range(PIECES)])
+            start(load_g(own))
+
+    run_pass(0, 7, None, (), None, (6, 1))
+
+    def plain(t, carry):
+        run_pass(t, 7 - t, 8 - t, (), 4, (6 - t, 1))
+        return carry
+
+    lax.fori_loop(1, 5, plain, 0)
+    for t in range(5, len(PASSES)):
+        given, own = PASSES[t]
+        after = None if given is None else (given - 1, 1) if given > 0 else (0, 0)
+        run_pass(t, given, own, joins(own) if own else (), own if own else None, after)
+
+    for k in range(BATCHES):
+        wait(load_g(k))
+    ends = []
+    for m, b in enumerate((4, 2)):
+        for i in range(PIECES):
+            pass_on(b, i, b).wait_recv()
+        ends += start([pltpu.make_async_copy(came_ref.at[b], fin_v.at[m], fin_sem.at[m])])
 
     def outer(x_tile, out_tile):
         out_tile[...] = dot(x_tile[...], gw_v[...], ((0,), (0,))).astype(BF16)
@@ -564,11 +589,9 @@
         out_specs=[pl.BlockSpec((BY_W_TALL, columns), lambda j: (j, 0))],
     )(x_ref, part_ref)
 
-    ends = []
-    for m, b in enumerate(reversed(joins(0))):
-        for i in range(PIECES):
-            sent[b, i].wait_recv()
-        ends += start([pltpu.make_async_copy(came_ref.at[b], fin_v.at[m], fin_sem.at[m])])
+    for i in range(PIECES):
+        pass_on(1, i, 1).wait_recv()
+    ends += start([pltpu.make_async_copy(came_ref.at[1], fin_v.at[2], fin_sem.at[2])])
     wait(ends)
 
     def finish(j, carry):
@@ -581,13 +604,14 @@
 
     lax.fori_loop(0, steps, finish, 0)
     wait(start([pltpu.make_async_copy(fin_v.at[0], out_ref, fin_sem.at[0])]))
-    for copy in sent.values():
-        copy.wait_send()
+    for k in range(1, BATCHES):
+        for i in range(PIECES):
+            pass_on(k, i, k).wait_send()
 
 
 def scatter_call(n, z, w, xb, top, inv, lab):
     depth, columns = w.shape
-    half, wide = z.shape[1] // 2, 1024
+    half, wide = z.shape[1] // 2, 2048
     anywhere, vmem = pl.BlockSpec(memory_space=pl.ANY), pl.BlockSpec(memory_space=pltpu.VMEM)
     dma = pltpu.SemaphoreType.DMA
     moved = jax.ShapeDtypeStruct((BATCHES, half, depth), BF16)
@@ -645,11 +669,11 @@
     load = pltpu.make_async_copy(part_ref, part_v, part_sem.at[0])
     for copy in g_load:
         copy.start()
-    load.start()
     by_x_load = pltpu.make_async_copy(by_x_ref, by_x_v, part_sem.at[2])
-    by_x_load.start()
     for copy in g_load:
         copy.wait()
+    load.start()
+    by_x_load.start()
 
     def outer(x_tile, out_tile):
         out_tile[...] = dot(x_tile[...], g_v[...], ((0,), (0,))).astype(BF16)

time: 437 us -> 410 us (0.938)
  Pallas kernels: 432 us -> 405 us
    pallas_call x1, Pallas kernels: 170 us -> 150 us  [logits_call(): pl.pallas_call(functools.partial(logits_kernel, n), in_specs=[anywhere, a...]
    pallas_call x1, Pallas kernels: 200 us -> 193 us  [scatter_call(): pl.pallas_call(functools.partial(scatter_kernel, n), in_specs=[anywhere,...]
where the time goes in v5:
time: 410 us; the launch traced here: 409 us
  Pallas kernels  405 us (99%)
    pallas_call x1, Pallas kernels, scatter_call(): pl.pallas_call(functools.partial(scatter_kernel, n), in_specs=[anywhere,...  193 us
    pallas_call x1, Pallas kernels, logits_call(): pl.pallas_call(functools.partial(logits_kernel, n), in_specs=[anywhere, a...  150 us
    pallas_call x1, Pallas kernels, by_w_call(): pl.pallas_call(by_w_kernel, in_specs=[anywhere] * 4, out_specs=[anywhere]...  62.9 us

profile of v5, /device:TPU:0, one launch (start us, length us, event | category | flops | bytes accessed | tf_op | source)
XLA Modules:
  0.0 409.0 jit_solution(10827621306691575347)
XLA Ops:
  0.6 0.8 reshape.22
  1.4 0.6 pad.4.lab_ref
  2.0 150.0 %gather_logits.1 = (bf16[8,384,6144]{2,1,0:T(8,128)(2,1)}, f32[8,384,2048]{2,1,0:T(8,128)}, f32[24,128]{1,0:T(8,128)}, f32[24,128]{1,0:T(8,128)}, f32[24,128]{1,0:T(8,128)}, /*index=5*/f32[24,128]{1,0:T(8,128)}) custom-call(bf16[192,6144]{1,0:T(8,128)(2,1)} %x_ref.1, bf16[6144,2048]{1,0:T(8,128)(2,1)} %w_ref.3, s32[3,128]{1,0:T(4,128)} %pad.4.lab_ref), custom_call_target="tpu_custom_call" | custom-call | flops 77309411328 | bytes 134217728 | tf_op jit(solution)/shard_map/gather_logits/pallas_call | solution.py:315
  152.0 0.8 reshape.23
  152.8 0.1 reshape.24
  152.9 0.6 constant_dynamic-slice_fusion
  153.4 192.6 %by_x_scatter.1 = (bf16[192,6144]{1,0:T(8,128)(2,1)}, bf16[8,384,2048]{2,1,0:T(8,128)(2,1)}, bf16[2560,2048]{1,0:T(8,128)(2,1)}, bf16[8,192,6144]{2,1,0:T(8,128)...) custom-call(f32[8,384,2048]{2,1,0:T(8,128)} %get-tuple-element.16.z_ref, bf16[6144,2048]{1,0:T(8,128)(2,1)} %w_ref.3, ...), custom_call_target="tpu_custom_call" | custom-call | flops 115964116992 | bytes 268435456 | tf_op jit(solution)/shard_map/by_x_scatter/pallas_call | solution.py:619
  346.0 62.9 %by_w.1 = (bf16[6144,2048]{1,0:T(8,128)(2,1)}, bf16[192,6144]{1,0:T(8,128)(2,1)}) custom-call(bf16[3072,6144]{1,0:T(8,128)(2,1)} %bitcast.9, bf16[3072,2048]{1,0:T(8,128)(2,1)} %bitcast.10, bf16[2560,2048]{1,0:T(8,128)(2,1)} %get-tuple-element.21.part_ref, bf16[192,6144]{1,0:T(8,128)(2,1)} %get-tuple-element.22.by_x_ref), custom_call_target="tpu_custom_call" | custom-call | flops 38654705664 | bytes 67108864 | tf_op jit(solution)/shard_map/by_w/pallas_call | solution.py:709
  (1 shorter events, 0.0 us)

commit v6 on v5

--- a/solution.py
+++ b/solution.py
@@ -431,6 +431,43 @@
         which = [(given, 1)] if own is None else [(own, 0)] if given is None else [(given, 1), (own, 0)]
         rows = half * len(which)
         g_copies = []
+        arrivals = [] if own is None else [took_ref.at[own]] + [came_ref.at[b] for b in joined]
+
+        def load_in(j, slot):
+            return [
+                pltpu.make_async_copy(ref.at[:, columns_at(j)], in_v.at[slot, m], in_sem.at[slot, m])
+                for m, ref in enumerate(arrivals)
+            ]
+
+        def slot_at(j):
+            return lax.rem(jnp.int32(t) * steps + j, 2)
+
+        def take_in():
+            if own is None:
+                return
+            partner = pltpu.make_async_remote_copy(
+                src_ref=took_ref.at[own],
+                dst_ref=took_ref.at[own],
+                send_sem=p_sem.at[0],
+                recv_sem=pair_recv.at[own],
+                device_id={"tp": flip(me, 1)},
+                device_id_type=MESH,
+            )
+            partner.wait_recv()
+            for b in joined:
+                for i in range(PIECES):
+                    pass_on(b, i, b).wait_recv()
+            start(load_in(0, slot_at(0)))
+            before = lax.rem(jnp.int32(t) * steps + 1, 2)
+            pltpu.make_async_remote_copy(
+                src_ref=p_v.at[before],
+                dst_ref=took_ref.at[own, :, columns_at(0)],
+                send_sem=p_sem.at[before],
+                recv_sem=pair_recv.at[own],
+                device_id={"tp": flip(me, 1)},
+                device_id_type=MESH,
+            ).wait_send()
+
         for place, (k, other) in enumerate(which):
             slot = 0 if own is None else 1 - place
             for i in range(PIECES):
@@ -454,6 +491,8 @@
                 return carry
 
             lax.fori_loop(0, half // 32, body, 0)
+            if place == 0:
+                take_in()
             for i in range(PIECES):
                 g_copies.append(
                     pltpu.make_async_copy(
@@ -463,28 +502,6 @@
                     )
                 )
         start(g_copies)
-
-        arrivals = []
-        if own is not None:
-            pltpu.make_async_remote_copy(
-                src_ref=took_ref.at[own],
-                dst_ref=took_ref.at[own],
-                send_sem=p_sem.at[0],
-                recv_sem=pair_recv.at[own],
-                device_id={"tp": flip(me, 1)},
-                device_id_type=MESH,
-            ).wait_recv()
-            arrivals.append(took_ref.at[own])
-            for b in joined:
-                for i in range(PIECES):
-                    pass_on(b, i, b).wait_recv()
-                arrivals.append(came_ref.at[b])
-
-        def load_in(j, slot):
-            return [
-                pltpu.make_async_copy(ref.at[:, columns_at(j)], in_v.at[slot, m], in_sem.at[slot, m])
-                for m, ref in enumerate(arrivals)
-            ]
 
         def outs(j, slot):
             copies = []
@@ -510,11 +527,6 @@
                 else:
                     copy.wait()
 
-        def slot_at(j):
-            return lax.rem(jnp.int32(t) * steps + j, 2)
-
-        start(load_in(0, slot_at(0)))
-
         def multiply(j, carry):
             slot = slot_at(j)
             if not final:
@@ -550,9 +562,9 @@
             return carry
 
         lax.fori_loop(0, steps, multiply, 0)
-        start(outs(steps - 1, slot_at(steps - 1)))
-        for j in (steps - 2, steps - 1):
-            finished(outs(j, slot_at(j)))
+        ending = start(outs(steps - 1, slot_at(steps - 1)))
+        finished(outs(steps - 2, slot_at(steps - 2)))
+        wait(ending if given is None else ending[1:])
         wait(g_copies)
         if own is not None:
             if not final:

time: 410 us -> 404 us (0.985)
  Pallas kernels: 405 us -> 399 us
    pallas_call x1, Pallas kernels: 193 us -> 187 us  [scatter_call(): pl.pallas_call(functools.partial(scatter_kernel, n), in_specs=[anywhere,...]
where the time goes in v6:
time: 404 us; the launch traced here: 403 us
  Pallas kernels  399 us (99%)
    pallas_call x1, Pallas kernels, scatter_call(): pl.pallas_call(functools.partial(scatter_kernel, n), in_specs=[anywhere,...  187 us
    pallas_call x1, Pallas kernels, logits_call(): pl.pallas_call(functools.partial(logits_kernel, n), in_specs=[anywhere, a...  150 us
    pallas_call x1, Pallas kernels, by_w_call(): pl.pallas_call(by_w_kernel, in_specs=[anywhere] * 4, out_specs=[anywhere]...  62.9 us

profile of v6, /device:TPU:0, one launch (start us, length us, event | category | flops | bytes accessed | tf_op | source)
XLA Modules:
  0.0 403.0 jit_solution(1569727510067199120)
XLA Ops:
  0.6 0.8 reshape.22
  1.4 0.6 pad.4.lab_ref
  2.0 150.0 %gather_logits.1 = (bf16[8,384,6144]{2,1,0:T(8,128)(2,1)}, f32[8,384,2048]{2,1,0:T(8,128)}, f32[24,128]{1,0:T(8,128)}, f32[24,128]{1,0:T(8,128)}, f32[24,128]{1,0:T(8,128)}, /*index=5*/f32[24,128]{1,0:T(8,128)}) custom-call(bf16[192,6144]{1,0:T(8,128)(2,1)} %x_ref.1, bf16[6144,2048]{1,0:T(8,128)(2,1)} %w_ref.3, s32[3,128]{1,0:T(4,128)} %pad.4.lab_ref), custom_call_target="tpu_custom_call" | custom-call | flops 77309411328 | bytes 134217728 | tf_op jit(solution)/shard_map/gather_logits/pallas_call | solution.py:315
  152.0 0.8 reshape.23
  152.8 0.1 reshape.24
  152.9 0.6 constant_dynamic-slice_fusion
  153.4 186.5 %by_x_scatter.1 = (bf16[192,6144]{1,0:T(8,128)(2,1)}, bf16[8,384,2048]{2,1,0:T(8,128)(2,1)}, bf16[2560,2048]{1,0:T(8,128)(2,1)}, bf16[8,192,6144]{2,1,0:T(8,128)...) custom-call(f32[8,384,2048]{2,1,0:T(8,128)} %get-tuple-element.16.z_ref, bf16[6144,2048]{1,0:T(8,128)(2,1)} %w_ref.3, ...), custom_call_target="tpu_custom_call" | custom-call | flops 115964116992 | bytes 268435456 | tf_op jit(solution)/shard_map/by_x_scatter/pallas_call | solution.py:631
  340.0 62.9 %by_w.1 = (bf16[6144,2048]{1,0:T(8,128)(2,1)}, bf16[192,6144]{1,0:T(8,128)(2,1)}) custom-call(bf16[3072,6144]{1,0:T(8,128)(2,1)} %bitcast.9, bf16[3072,2048]{1,0:T(8,128)(2,1)} %bitcast.10, bf16[2560,2048]{1,0:T(8,128)(2,1)} %get-tuple-element.21.part_ref, bf16[192,6144]{1,0:T(8,128)(2,1)} %get-tuple-element.22.by_x_ref), custom_call_target="tpu_custom_call" | custom-call | flops 38654705664 | bytes 67108864 | tf_op jit(solution)/shard_map/by_w/pallas_call | solution.py:721
  (1 shorter events, 0.0 us)
